TPU v7x, 128 devices: a whole 4x4x4 slice. The times are simulated.
128 devices in a mesh: col: 2 (over core), row: 64 (over z, y, x).
Axes of the slice: x: 4, y: 4, z: 4, core: 2. Of those that a mesh axis runs over, the one named last changes fastest.
Arguments:
- forcing: float32 [2, 1536, 48, 256], P(None, 'row', 'col')
- init_guess: float32 [2, 1536, 48, 256], P(None, 'row', 'col')
- cell_coef: float32 [2, 1536, 48], P(None, 'row', 'col')
- solve_rows: bfloat16 [2, 64, 2, 576, 784], P(None, 'row', 'col')
- relax_factor: float32 [2], replicated
Outputs:
- output: float32 [2, 1536, 48, 256], P(None, 'row', 'col')
All inputs are finite; a program needn't handle non-finite values.
Results may differ from a plain program's by a relative error of at most 0.001.
Values are sent between devices in bfloat16 or wider.
A program may use at most 1 GiB of HBM per device.

v0:
```python
import math
import jax
import jax.numpy as jnp
from jax import lax
from jax.sharding import PartitionSpec as P

SWEEPS = 4


def up_perm(axis_size):
    return [(device, device + 1) for device in range(axis_size - 1)]


def down_perm(axis_size):
    return [(device + 1, device) for device in range(axis_size - 1)]


def grow_halo(values, halo_width, grid_dim, axis_name, axis_size):
    extent = values.shape[grid_dim]
    low_edge = lax.slice_in_dim(values, 0, halo_width, axis=grid_dim)
    high_edge = lax.slice_in_dim(values, extent - halo_width, extent, axis=grid_dim)
    from_below = lax.ppermute(high_edge, axis_name, up_perm(axis_size))
    from_above = lax.ppermute(low_edge, axis_name, down_perm(axis_size))
    return jnp.concatenate([from_below, values, from_above], axis=grid_dim)


def edge_faces(coef_grid, grid_dim, axis_name, axis_size):
    position = lax.axis_index(axis_name)
    extent = coef_grid.shape[grid_dim]
    low_edge = lax.slice_in_dim(coef_grid, 0, 1, axis=grid_dim)
    high_edge = lax.slice_in_dim(coef_grid, extent - 1, extent, axis=grid_dim)
    from_below = lax.ppermute(high_edge, axis_name, up_perm(axis_size))
    from_above = lax.ppermute(low_edge, axis_name, down_perm(axis_size))
    low_side = jnp.where(position == 0, low_edge, from_below)
    high_side = jnp.where(position == axis_size - 1, high_edge, from_above)
    widened = jnp.concatenate([low_side, coef_grid, high_side], axis=grid_dim)
    return 0.5 * (lax.slice_in_dim(widened, 0, extent + 1, axis=grid_dim) + lax.slice_in_dim(widened, 1, extent + 2, axis=grid_dim))


def apply_local(face_x, face_y, wide_x, wide_y):
    flux_x = face_x[..., None] * (wide_x[:, 1:] - wide_x[:, :-1])
    flux_y = face_y[..., None] * (wide_y[:, :, 1:] - wide_y[:, :, :-1])
    return flux_x[:, :-1] - flux_x[:, 1:] + flux_y[:, :, :-1] - flux_y[:, :, 1:]


def solution(mesh):
    row_count = mesh.shape["row"]
    col_count = mesh.shape["col"]
    grid_spec = P(None, "row", "col", None)

    def local_sweeps(forcing, init_guess, cell_coef, solve_rows, relax_factor):
        num_sys, sub_size, _, num_rhs = forcing.shape
        ext_size = math.isqrt(solve_rows.shape[-1])
        margin = (ext_size - sub_size) // 2
        solve_mat = solve_rows.reshape(num_sys, sub_size * sub_size, ext_size * ext_size)
        step_size = relax_factor[:, None, None, None]
        face_x = edge_faces(cell_coef, 1, "row", row_count)
        face_y = edge_faces(cell_coef, 2, "col", col_count)

        def apply_op(values):
            return apply_local(face_x, face_y, grow_halo(values, 1, 1, "row", row_count), grow_halo(values, 1, 2, "col", col_count))

        residual = forcing - apply_op(init_guess)
        approx = init_guess
        for _ in range(SWEEPS):
            low_res = residual.astype(jnp.bfloat16)
            window = grow_halo(grow_halo(low_res, margin, 1, "row", row_count), margin, 2, "col", col_count)
            correction = jnp.einsum("sqe,sek->sqk", solve_mat, window.reshape(num_sys, ext_size * ext_size, num_rhs), preferred_element_type=jnp.float32)
            correction = correction.reshape(num_sys, sub_size, sub_size, num_rhs)
            approx = approx + step_size * correction
            residual = residual - step_size * apply_op(correction)
        return approx

    return jax.shard_map(local_sweeps, mesh=mesh, in_specs=(grid_spec, grid_spec, P(None, "row", "col"), P(None, "row", "col", None, None), P(None)), out_specs=grid_spec, check_vma=False)
```

profile of v0, /device:TPU:97, one launch (start us, length us, event | category | flops | bytes accessed | tf_op | source)
XLA Modules:
  0.0 171.2 jit_solution(14082165484154132012)
XLA Ops:
  0.9 6.7 %collective-permute-start.1 = (f32[2,1,24]{2,1,0:T(1,128)S(1)}, f32[2,1,24]{2,1,0:T(1,128)S(1)}, u32[]{:S(2)}, u32[]{:S(2)}) collective-permute-start(f32[2,1,24]{2,1,0:T(1,128)S(1)} %get-tuple-element.45), channel_id=1, source_target_pairs={{1,0},{2,1},{3,2},{4,3},{5,4},{6,5},{7,6},{8,7},{9,8},{10,9},{11,1... | collective-permute-start | bytes 584 | tf_op jit(solution)/shard_map/ppermute | solution.py:33
  7.5 1.9 %collective-permute-start = (f32[2,1,24]{2,1,0:T(1,128)S(1)}, f32[2,1,24]{2,1,0:T(1,128)S(1)}, u32[]{:S(2)}, u32[]{:S(2)}) collective-permute-start(f32[2,1,24]{2,1,0:T(1,128)S(1)} %get-tuple-element.46), channel_id=1, source_target_pairs={{0,1},{1,2},{2,3},{3,4},{4,5},{5,6},{6,7},{7,8},{8,9},{9,10},{10,1... | collective-permute-start | bytes 584 | tf_op jit(solution)/shard_map/ppermute | solution.py:32
  10.4 2.9 %collective-permute-start.5 = (f32[2,24,1]{2,1,0:T(8,128)S(1)}, f32[2,24,1]{2,1,0:T(8,128)S(1)}, u32[]{:S(2)}, u32[]{:S(2)}) collective-permute-start(f32[2,24,1]{2,1,0:T(8,128)S(1)} %get-tuple-element.49), channel_id=1, source_target_pairs={{64,0},{65,1},{66,2},{67,3},{68,4},{69,5},{70,6},{71,7},{72,8},{73... | collective-permute-start | bytes 584 | tf_op jit(solution)/shard_map/ppermute | solution.py:33
  13.2 1.3 collective-permute-start.4
  15.4 1.9 %collective-permute-start.3 = (f32[2,1,24,256]{3,2,1,0:T(8,128)S(1)}, f32[2,1,24,256]{3,2,1,0:T(8,128)S(1)}, u32[]{:S(2)}, u32[]{:S(2)}) collective-permute-start(f32[2,1,24,256]{3,2,1,0:T(8,128)S(1)} %get-tuple-element.23), channel_id=1, source_target_pairs={{0,1},{1,2},{2,3},{3,4},{4,5},{5,6},{6,7},{7,8},{8,9},{9,10},{10,1... | collective-permute-start | bytes 147464 | tf_op jit(solution)/shard_map/ppermute | solution.py:22
  17.3 1.2 fusion.41
  18.5 7.9 %collective-permute-start.2 = (f32[2,1,24,256]{3,2,1,0:T(8,128)S(1)}, f32[2,1,24,256]{3,2,1,0:T(8,128)S(1)}, u32[]{:S(2)}, u32[]{:S(2)}) collective-permute-start(f32[2,1,24,256]{3,2,1,0:T(8,128)S(1)} %get-tuple-element.24), channel_id=1, source_target_pairs={{1,0},{2,1},{3,2},{4,3},{5,4},{6,5},{7,6},{8,7},{9,8},{10,9},{11,1... | collective-permute-start | bytes 147464 | tf_op jit(solution)/shard_map/ppermute | solution.py:23
  26.4 1.3 collective-permute-start.7
  29.2 3.3 %collective-permute-start.6 = (f32[2,24,1,256]{3,2,1,0:T(1,128)S(1)}, f32[2,24,1,256]{3,2,1,0:T(1,128)S(1)}, u32[]{:S(2)}, u32[]{:S(2)}) collective-permute-start(f32[2,24,1,256]{3,2,1,0:T(1,128)S(1)} %get-tuple-element.26), channel_id=1, source_target_pairs={{64,0},{65,1},{66,2},{67,3},{68,4},{69,5},{70,6},{71,7},{72,8},{73... | collective-permute-start | bytes 147464 | tf_op jit(solution)/shard_map/ppermute | solution.py:23
  34.4 2.1 %fusion.12 = f32[2,25,24,256]{3,2,1,0:T(8,128)S(1)} fusion(f32[2,1,24,256]{3,2,1,0:T(8,128)S(1)} %collective-permute-done.2, f32[2,24,24,256]{3,2,1,0:T(8,128)} %param.6, f32[2,1,24,256]{3,2,1,0:T(8,128)S(1)} %collective-permute-done.3, f32[2,25,24]{2,1,0:T(8,128)S(1)} %fusion.26), kind=kLoop, calls=%fused_computation.17 | loop fusion | flops 1228800 | bytes 2511552 | tf_op jit(solution)/shard_map/mul | solution.py:41
  38.2 1.9 %collective-permute-start.8 = (bf16[2,2,24,256]{3,2,1,0:T(8,128)(2,1)S(1)}, bf16[2,2,24,256]{3,2,1,0:T(8,128)(2,1)S(1)}, u32[]{:S(2)}, u32[]{:S(2)}) collective-permute-start(bf16[2,2,24,256]{3,2,1,0:T(8,128)(2,1)S(1)} %get-tuple-element.41), channel_id=1, source_target_pairs={{0,1},{1,2},{2,3},{3,4},{4,5},{5,6},{6,7},{7,8},{8,9},{9,10},{10,1... | collective-permute-start | bytes 147464 | tf_op jit(solution)/shard_map/ppermute | solution.py:22
  40.1 7.6 %collective-permute-start.9 = (bf16[2,2,24,256]{3,2,1,0:T(8,128)(2,1)S(1)}, bf16[2,2,24,256]{3,2,1,0:T(8,128)(2,1)S(1)}, u32[]{:S(2)}, u32[]{:S(2)}) collective-permute-start(bf16[2,2,24,256]{3,2,1,0:T(8,128)(2,1)S(1)} %get-tuple-element.42), channel_id=1, source_target_pairs={{1,0},{2,1},{3,2},{4,3},{5,4},{6,5},{7,6},{8,7},{9,8},{10,9},{11,1... | collective-permute-start | bytes 147464 | tf_op jit(solution)/shard_map/ppermute | solution.py:23
  47.8 1.3 collective-permute-done.9
  49.2 1.3 collective-permute-start.10
  50.5 3.0 %collective-permute-start.11 = (bf16[2,28,2,256]{3,2,1,0:T(2,128)(2,1)S(1)}, bf16[2,28,2,256]{3,2,1,0:T(2,128)(2,1)S(1)}, u32[]{:S(2)}, u32[]{:S(2)}) collective-permute-start(bf16[2,28,2,256]{3,2,1,0:T(2,128)(2,1)S(1)} %get-tuple-element.34), channel_id=1, source_target_pairs={{64,0},{65,1},{66,2},{67,3},{68,4},{69,5},{70,6},{71,7},{72,8},{73... | collective-permute-start | bytes 172040 | tf_op jit(solution)/shard_map/ppermute | solution.py:23
  56.8 1.9 %collective-permute-start.13 = (f32[2,1,24,256]{3,2,1,0:T(8,128)S(1)}, f32[2,1,24,256]{3,2,1,0:T(8,128)S(1)}, u32[]{:S(2)}, u32[]{:S(2)}) collective-permute-start(f32[2,1,24,256]{3,2,1,0:T(8,128)S(1)} %get-tuple-element.19), channel_id=1, source_target_pairs={{0,1},{1,2},{2,3},{3,4},{4,5},{5,6},{6,7},{7,8},{8,9},{9,10},{10,1... | collective-permute-start | bytes 147464 | tf_op jit(solution)/shard_map/ppermute | solution.py:22
  58.7 8.3 %collective-permute-start.12 = (f32[2,1,24,256]{3,2,1,0:T(8,128)S(1)}, f32[2,1,24,256]{3,2,1,0:T(8,128)S(1)}, u32[]{:S(2)}, u32[]{:S(2)}) collective-permute-start(f32[2,1,24,256]{3,2,1,0:T(8,128)S(1)} %get-tuple-element.20), channel_id=1, source_target_pairs={{1,0},{2,1},{3,2},{4,3},{5,4},{6,5},{7,6},{8,7},{9,8},{10,9},{11,1... | collective-permute-start | bytes 147464 | tf_op jit(solution)/shard_map/ppermute | solution.py:23
  67.2 1.3 collective-permute-start.15
  68.5 3.0 %collective-permute-start.14 = (f32[2,24,1,256]{3,2,1,0:T(1,128)S(1)}, f32[2,24,1,256]{3,2,1,0:T(1,128)S(1)}, u32[]{:S(2)}, u32[]{:S(2)}) collective-permute-start(f32[2,24,1,256]{3,2,1,0:T(1,128)S(1)} %get-tuple-element.22), channel_id=1, source_target_pairs={{64,0},{65,1},{66,2},{67,3},{68,4},{69,5},{70,6},{71,7},{72,8},{73... | collective-permute-start | bytes 147464 | tf_op jit(solution)/shard_map/ppermute | solution.py:23
  73.2 1.9 %collective-permute-start.16 = (bf16[2,2,24,256]{3,2,1,0:T(8,128)(2,1)S(1)}, bf16[2,2,24,256]{3,2,1,0:T(8,128)(2,1)S(1)}, u32[]{:S(2)}, u32[]{:S(2)}) collective-permute-start(bf16[2,2,24,256]{3,2,1,0:T(8,128)(2,1)S(1)} %get-tuple-element.39), channel_id=1, source_target_pairs={{0,1},{1,2},{2,3},{3,4},{4,5},{5,6},{6,7},{7,8},{8,9},{9,10},{10,1... | collective-permute-start | bytes 147464 | tf_op jit(solution)/shard_map/ppermute | solution.py:22
  75.1 7.6 %collective-permute-start.17 = (bf16[2,2,24,256]{3,2,1,0:T(8,128)(2,1)S(1)}, bf16[2,2,24,256]{3,2,1,0:T(8,128)(2,1)S(1)}, u32[]{:S(2)}, u32[]{:S(2)}) collective-permute-start(bf16[2,2,24,256]{3,2,1,0:T(8,128)(2,1)S(1)} %get-tuple-element.40), channel_id=1, source_target_pairs={{1,0},{2,1},{3,2},{4,3},{5,4},{6,5},{7,6},{8,7},{9,8},{10,9},{11,1... | collective-permute-start | bytes 147464 | tf_op jit(solution)/shard_map/ppermute | solution.py:23
  82.7 1.1 collective-permute-done.17
  83.9 1.3 collective-permute-start.18
  85.2 3.4 %collective-permute-start.19 = (bf16[2,28,2,256]{3,2,1,0:T(2,128)(2,1)S(1)}, bf16[2,28,2,256]{3,2,1,0:T(2,128)(2,1)S(1)}, u32[]{:S(2)}, u32[]{:S(2)}) collective-permute-start(bf16[2,28,2,256]{3,2,1,0:T(2,128)(2,1)S(1)} %get-tuple-element.32), channel_id=1, source_target_pairs={{64,0},{65,1},{66,2},{67,3},{68,4},{69,5},{70,6},{71,7},{72,8},{73... | collective-permute-start | bytes 172040 | tf_op jit(solution)/shard_map/ppermute | solution.py:23
  91.9 1.9 %collective-permute-start.21 = (f32[2,1,24,256]{3,2,1,0:T(8,128)S(1)}, f32[2,1,24,256]{3,2,1,0:T(8,128)S(1)}, u32[]{:S(2)}, u32[]{:S(2)}) collective-permute-start(f32[2,1,24,256]{3,2,1,0:T(8,128)S(1)} %get-tuple-element.15), channel_id=1, source_target_pairs={{0,1},{1,2},{2,3},{3,4},{4,5},{5,6},{6,7},{7,8},{8,9},{9,10},{10,1... | collective-permute-start | bytes 147464 | tf_op jit(solution)/shard_map/ppermute | solution.py:22
  93.9 8.2 %collective-permute-start.20 = (f32[2,1,24,256]{3,2,1,0:T(8,128)S(1)}, f32[2,1,24,256]{3,2,1,0:T(8,128)S(1)}, u32[]{:S(2)}, u32[]{:S(2)}) collective-permute-start(f32[2,1,24,256]{3,2,1,0:T(8,128)S(1)} %get-tuple-element.16), channel_id=1, source_target_pairs={{1,0},{2,1},{3,2},{4,3},{5,4},{6,5},{7,6},{8,7},{9,8},{10,9},{11,1... | collective-permute-start | bytes 147464 | tf_op jit(solution)/shard_map/ppermute | solution.py:23
  102.1 1.3 collective-permute-start.23
  103.4 3.0 %collective-permute-start.22 = (f32[2,24,1,256]{3,2,1,0:T(1,128)S(1)}, f32[2,24,1,256]{3,2,1,0:T(1,128)S(1)}, u32[]{:S(2)}, u32[]{:S(2)}) collective-permute-start(f32[2,24,1,256]{3,2,1,0:T(1,128)S(1)} %get-tuple-element.18), channel_id=1, source_target_pairs={{64,0},{65,1},{66,2},{67,3},{68,4},{69,5},{70,6},{71,7},{72,8},{73... | collective-permute-start | bytes 147464 | tf_op jit(solution)/shard_map/ppermute | solution.py:23
  107.7 1.4 fusion.28
  109.1 1.9 %collective-permute-start.24 = (bf16[2,2,24,256]{3,2,1,0:T(8,128)(2,1)S(1)}, bf16[2,2,24,256]{3,2,1,0:T(8,128)(2,1)S(1)}, u32[]{:S(2)}, u32[]{:S(2)}) collective-permute-start(bf16[2,2,24,256]{3,2,1,0:T(8,128)(2,1)S(1)} %get-tuple-element.37), channel_id=1, source_target_pairs={{0,1},{1,2},{2,3},{3,4},{4,5},{5,6},{6,7},{7,8},{8,9},{9,10},{10,1... | collective-permute-start | bytes 147464 | tf_op jit(solution)/shard_map/ppermute | solution.py:22
  111.1 7.6 %collective-permute-start.25 = (bf16[2,2,24,256]{3,2,1,0:T(8,128)(2,1)S(1)}, bf16[2,2,24,256]{3,2,1,0:T(8,128)(2,1)S(1)}, u32[]{:S(2)}, u32[]{:S(2)}) collective-permute-start(bf16[2,2,24,256]{3,2,1,0:T(8,128)(2,1)S(1)} %get-tuple-element.38), channel_id=1, source_target_pairs={{1,0},{2,1},{3,2},{4,3},{5,4},{6,5},{7,6},{8,7},{9,8},{10,9},{11,1... | collective-permute-start | bytes 147464 | tf_op jit(solution)/shard_map/ppermute | solution.py:23
  119.9 1.3 collective-permute-start.26
  121.2 3.6 %collective-permute-start.27 = (bf16[2,28,2,256]{3,2,1,0:T(2,128)(2,1)S(1)}, bf16[2,28,2,256]{3,2,1,0:T(2,128)(2,1)S(1)}, u32[]{:S(2)}, u32[]{:S(2)}) collective-permute-start(bf16[2,28,2,256]{3,2,1,0:T(2,128)(2,1)S(1)} %get-tuple-element.30), channel_id=1, source_target_pairs={{64,0},{65,1},{66,2},{67,3},{68,4},{69,5},{70,6},{71,7},{72,8},{73... | collective-permute-start | bytes 172040 | tf_op jit(solution)/shard_map/ppermute | solution.py:23
  125.5 1.5 pad_maximum_fusion.2
  127.0 2.0 %reshape.35 = bf16[2,784,256]{2,1,0:T(8,128)(2,1)} reshape(bf16[2,28,28,256]{3,2,1,0:T(8,128)(2,1)} %pad_maximum_fusion.2) | data formatting | bytes 1605632 | tf_op jit(solution)/shard_map/reshape | solution.py:68
  129.0 2.1 %fusion.2 = f32[2,256,576]{1,2,0:T(8,128)S(1)} fusion(bf16[2,784,256]{2,1,0:T(8,128)(2,1)} %reshape.35, bf16[2,1,1,576,784]{3,4,2,1,0:T(8,128)(2,1)S(1)} %copy-done), kind=kOutput, calls=%fused_computation.2 | convolution fusion | flops 462422016 | bytes 3788800 | tf_op jit(solution)/shard_map/sqe,sek->sqk/dot_general | solution.py:68
  131.2 1.9 %collective-permute-start.29 = (f32[2,1,24,256]{3,2,1,0:T(8,128)S(1)}, f32[2,1,24,256]{3,2,1,0:T(8,128)S(1)}, u32[]{:S(2)}, u32[]{:S(2)}) collective-permute-start(f32[2,1,24,256]{3,2,1,0:T(8,128)S(1)} %get-tuple-element.11), channel_id=1, source_target_pairs={{0,1},{1,2},{2,3},{3,4},{4,5},{5,6},{6,7},{7,8},{8,9},{9,10},{10,1... | collective-permute-start | bytes 147464 | tf_op jit(solution)/shard_map/ppermute | solution.py:22
  133.1 8.2 %collective-permute-start.28 = (f32[2,1,24,256]{3,2,1,0:T(8,128)S(1)}, f32[2,1,24,256]{3,2,1,0:T(8,128)S(1)}, u32[]{:S(2)}, u32[]{:S(2)}) collective-permute-start(f32[2,1,24,256]{3,2,1,0:T(8,128)S(1)} %get-tuple-element.12), channel_id=1, source_target_pairs={{1,0},{2,1},{3,2},{4,3},{5,4},{6,5},{7,6},{8,7},{9,8},{10,9},{11,1... | collective-permute-start | bytes 147464 | tf_op jit(solution)/shard_map/ppermute | solution.py:23
  141.4 1.3 collective-permute-start.31
  142.7 3.0 %collective-permute-start.30 = (f32[2,24,1,256]{3,2,1,0:T(1,128)S(1)}, f32[2,24,1,256]{3,2,1,0:T(1,128)S(1)}, u32[]{:S(2)}, u32[]{:S(2)}) collective-permute-start(f32[2,24,1,256]{3,2,1,0:T(1,128)S(1)} %get-tuple-element.14), channel_id=1, source_target_pairs={{64,0},{65,1},{66,2},{67,3},{68,4},{69,5},{70,6},{71,7},{72,8},{73... | collective-permute-start | bytes 147464 | tf_op jit(solution)/shard_map/ppermute | solution.py:23
  147.8 1.9 %collective-permute-start.32 = (bf16[2,2,24,256]{3,2,1,0:T(8,128)(2,1)S(1)}, bf16[2,2,24,256]{3,2,1,0:T(8,128)(2,1)S(1)}, u32[]{:S(2)}, u32[]{:S(2)}) collective-permute-start(bf16[2,2,24,256]{3,2,1,0:T(8,128)(2,1)S(1)} %get-tuple-element.35), channel_id=1, source_target_pairs={{0,1},{1,2},{2,3},{3,4},{4,5},{5,6},{6,7},{7,8},{8,9},{9,10},{10,1... | collective-permute-start | bytes 147464 | tf_op jit(solution)/shard_map/ppermute | solution.py:22
  149.7 7.6 %collective-permute-start.33 = (bf16[2,2,24,256]{3,2,1,0:T(8,128)(2,1)S(1)}, bf16[2,2,24,256]{3,2,1,0:T(8,128)(2,1)S(1)}, u32[]{:S(2)}, u32[]{:S(2)}) collective-permute-start(bf16[2,2,24,256]{3,2,1,0:T(8,128)(2,1)S(1)} %get-tuple-element.36), channel_id=1, source_target_pairs={{1,0},{2,1},{3,2},{4,3},{5,4},{6,5},{7,6},{8,7},{9,8},{10,9},{11,1... | collective-permute-start | bytes 147464 | tf_op jit(solution)/shard_map/ppermute | solution.py:23
  158.6 1.3 collective-permute-start.34
  159.9 3.1 %collective-permute-start.35 = (bf16[2,28,2,256]{3,2,1,0:T(2,128)(2,1)S(1)}, bf16[2,28,2,256]{3,2,1,0:T(2,128)(2,1)S(1)}, u32[]{:S(2)}, u32[]{:S(2)}) collective-permute-start(bf16[2,28,2,256]{3,2,1,0:T(2,128)(2,1)S(1)} %get-tuple-element.28), channel_id=1, source_target_pairs={{64,0},{65,1},{66,2},{67,3},{68,4},{69,5},{70,6},{71,7},{72,8},{73... | collective-permute-start | bytes 172040 | tf_op jit(solution)/shard_map/ppermute | solution.py:23
  163.8 1.5 pad_maximum_fusion.3
  165.3 2.1 %reshape.37 = bf16[2,784,256]{2,1,0:T(8,128)(2,1)} reshape(bf16[2,28,28,256]{3,2,1,0:T(8,128)(2,1)} %pad_maximum_fusion.3) | data formatting | bytes 1605632 | tf_op jit(solution)/shard_map/reshape | solution.py:68
  167.4 2.3 %fusion = f32[2,256,576]{1,2,0:T(8,128)S(1)} fusion(bf16[2,784,256]{2,1,0:T(8,128)(2,1)} %reshape.37, bf16[2,1,1,576,784]{3,4,2,1,0:T(8,128)(2,1)S(1)} %copy-done), kind=kOutput, calls=%fused_computation | convolution fusion | flops 462422016 | bytes 3788800 | tf_op jit(solution)/shard_map/sqe,sek->sqk/dot_general | solution.py:68
  169.7 1.5 multiply_add_fusion
  (91 shorter events, 23.4 us)
Async XLA Ops:
  0.0 55.8 %copy-start = (bf16[2,1,1,576,784]{3,4,2,1,0:T(8,128)(2,1)S(1)}, bf16[2,1,1,576,784]{3,4,2,1,0:T(8,128)(2,1)}, u32[]{:S(2)}) copy-start(bf16[2,1,1,576,784]{3,4,2,1,0:T(8,128)(2,1)} %param.8) | copy-start | bytes 5419012
  0.9 17.6 %collective-permute-start.1 = (f32[2,1,24]{2,1,0:T(1,128)S(1)}, f32[2,1,24]{2,1,0:T(1,128)S(1)}, u32[]{:S(2)}, u32[]{:S(2)}) collective-permute-start(f32[2,1,24]{2,1,0:T(1,128)S(1)} %get-tuple-element.45), channel_id=1, source_target_pairs={{1,0},{2,1},{3,2},{4,3},{5,4},{6,5},{7,6},{8,7},{9,8},{10,9},{11,1... | collective-permute-start | bytes 584 | tf_op jit(solution)/shard_map/ppermute | solution.py:33
  7.5 18.8 %collective-permute-start = (f32[2,1,24]{2,1,0:T(1,128)S(1)}, f32[2,1,24]{2,1,0:T(1,128)S(1)}, u32[]{:S(2)}, u32[]{:S(2)}) collective-permute-start(f32[2,1,24]{2,1,0:T(1,128)S(1)} %get-tuple-element.46), channel_id=1, source_target_pairs={{0,1},{1,2},{2,3},{3,4},{4,5},{5,6},{6,7},{7,8},{8,9},{9,10},{10,1... | collective-permute-start | bytes 584 | tf_op jit(solution)/shard_map/ppermute | solution.py:32
  10.4 18.9 %collective-permute-start.5 = (f32[2,24,1]{2,1,0:T(8,128)S(1)}, f32[2,24,1]{2,1,0:T(8,128)S(1)}, u32[]{:S(2)}, u32[]{:S(2)}) collective-permute-start(f32[2,24,1]{2,1,0:T(8,128)S(1)} %get-tuple-element.49), channel_id=1, source_target_pairs={{64,0},{65,1},{66,2},{67,3},{68,4},{69,5},{70,6},{71,7},{72,8},{73... | collective-permute-start | bytes 584 | tf_op jit(solution)/shard_map/ppermute | solution.py:33
  13.2 19.3 %collective-permute-start.4 = (f32[2,24,1]{2,1,0:T(8,128)S(1)}, f32[2,24,1]{2,1,0:T(8,128)S(1)}, u32[]{:S(2)}, u32[]{:S(2)}) collective-permute-start(f32[2,24,1]{2,1,0:T(8,128)S(1)} %get-tuple-element.50), channel_id=1, source_target_pairs={{0,64},{1,65},{2,66},{3,67},{4,68},{5,69},{6,70},{7,71},{8,72},{9,... | collective-permute-start | bytes 584 | tf_op jit(solution)/shard_map/ppermute | solution.py:32
  15.4 19.0 %collective-permute-start.3 = (f32[2,1,24,256]{3,2,1,0:T(8,128)S(1)}, f32[2,1,24,256]{3,2,1,0:T(8,128)S(1)}, u32[]{:S(2)}, u32[]{:S(2)}) collective-permute-start(f32[2,1,24,256]{3,2,1,0:T(8,128)S(1)} %get-tuple-element.23), channel_id=1, source_target_pairs={{0,1},{1,2},{2,3},{3,4},{4,5},{5,6},{6,7},{7,8},{8,9},{9,10},{10,1... | collective-permute-start | bytes 147464 | tf_op jit(solution)/shard_map/ppermute | solution.py:22
  18.5 15.9 %collective-permute-start.2 = (f32[2,1,24,256]{3,2,1,0:T(8,128)S(1)}, f32[2,1,24,256]{3,2,1,0:T(8,128)S(1)}, u32[]{:S(2)}, u32[]{:S(2)}) collective-permute-start(f32[2,1,24,256]{3,2,1,0:T(8,128)S(1)} %get-tuple-element.24), channel_id=1, source_target_pairs={{1,0},{2,1},{3,2},{4,3},{5,4},{6,5},{7,6},{8,7},{9,8},{10,9},{11,1... | collective-permute-start | bytes 147464 | tf_op jit(solution)/shard_map/ppermute | solution.py:23
  26.4 10.1 %collective-permute-start.7 = (f32[2,24,1,256]{3,2,1,0:T(1,128)S(1)}, f32[2,24,1,256]{3,2,1,0:T(1,128)S(1)}, u32[]{:S(2)}, u32[]{:S(2)}) collective-permute-start(f32[2,24,1,256]{3,2,1,0:T(1,128)S(1)} %get-tuple-element.25), channel_id=1, source_target_pairs={{0,64},{1,65},{2,66},{3,67},{4,68},{5,69},{6,70},{7,71},{8,72},{9,... | collective-permute-start | bytes 147464 | tf_op jit(solution)/shard_map/ppermute | solution.py:22
  29.2 7.3 %collective-permute-start.6 = (f32[2,24,1,256]{3,2,1,0:T(1,128)S(1)}, f32[2,24,1,256]{3,2,1,0:T(1,128)S(1)}, u32[]{:S(2)}, u32[]{:S(2)}) collective-permute-start(f32[2,24,1,256]{3,2,1,0:T(1,128)S(1)} %get-tuple-element.26), channel_id=1, source_target_pairs={{64,0},{65,1},{66,2},{67,3},{68,4},{69,5},{70,6},{71,7},{72,8},{73... | collective-permute-start | bytes 147464 | tf_op jit(solution)/shard_map/ppermute | solution.py:23
  34.3 2.2 %copy-start.5 = (f32[2,24,24,256]{3,2,1,0:T(8,128)S(1)}, f32[2,24,24,256]{3,2,1,0:T(8,128)}, u32[]{:S(2)}) copy-start(f32[2,24,24,256]{3,2,1,0:T(8,128)} %param.6) | copy-start | bytes 3538948
  36.5 1.3 copy-start.8
  38.2 9.6 %collective-permute-start.8 = (bf16[2,2,24,256]{3,2,1,0:T(8,128)(2,1)S(1)}, bf16[2,2,24,256]{3,2,1,0:T(8,128)(2,1)S(1)}, u32[]{:S(2)}, u32[]{:S(2)}) collective-permute-start(bf16[2,2,24,256]{3,2,1,0:T(8,128)(2,1)S(1)} %get-tuple-element.41), channel_id=1, source_target_pairs={{0,1},{1,2},{2,3},{3,4},{4,5},{5,6},{6,7},{7,8},{8,9},{9,10},{10,1... | collective-permute-start | bytes 147464 | tf_op jit(solution)/shard_map/ppermute | solution.py:22
  40.1 9.0 %collective-permute-start.9 = (bf16[2,2,24,256]{3,2,1,0:T(8,128)(2,1)S(1)}, bf16[2,2,24,256]{3,2,1,0:T(8,128)(2,1)S(1)}, u32[]{:S(2)}, u32[]{:S(2)}) collective-permute-start(bf16[2,2,24,256]{3,2,1,0:T(8,128)(2,1)S(1)} %get-tuple-element.42), channel_id=1, source_target_pairs={{1,0},{2,1},{3,2},{4,3},{5,4},{6,5},{7,6},{8,7},{9,8},{10,9},{11,1... | collective-permute-start | bytes 147464 | tf_op jit(solution)/shard_map/ppermute | solution.py:23
  49.2 4.3 %collective-permute-start.10 = (bf16[2,28,2,256]{3,2,1,0:T(2,128)(2,1)S(1)}, bf16[2,28,2,256]{3,2,1,0:T(2,128)(2,1)S(1)}, u32[]{:S(2)}, u32[]{:S(2)}) collective-permute-start(bf16[2,28,2,256]{3,2,1,0:T(2,128)(2,1)S(1)} %get-tuple-element.33), channel_id=1, source_target_pairs={{0,64},{1,65},{2,66},{3,67},{4,68},{5,69},{6,70},{7,71},{8,72},{9,... | collective-permute-start | bytes 172040 | tf_op jit(solution)/shard_map/ppermute | solution.py:22
  50.5 3.9 %collective-permute-start.11 = (bf16[2,28,2,256]{3,2,1,0:T(2,128)(2,1)S(1)}, bf16[2,28,2,256]{3,2,1,0:T(2,128)(2,1)S(1)}, u32[]{:S(2)}, u32[]{:S(2)}) collective-permute-start(bf16[2,28,2,256]{3,2,1,0:T(2,128)(2,1)S(1)} %get-tuple-element.34), channel_id=1, source_target_pairs={{64,0},{65,1},{66,2},{67,3},{68,4},{69,5},{70,6},{71,7},{72,8},{73... | collective-permute-start | bytes 172040 | tf_op jit(solution)/shard_map/ppermute | solution.py:23
  56.8 14.7 %collective-permute-start.13 = (f32[2,1,24,256]{3,2,1,0:T(8,128)S(1)}, f32[2,1,24,256]{3,2,1,0:T(8,128)S(1)}, u32[]{:S(2)}, u32[]{:S(2)}) collective-permute-start(f32[2,1,24,256]{3,2,1,0:T(8,128)S(1)} %get-tuple-element.19), channel_id=1, source_target_pairs={{0,1},{1,2},{2,3},{3,4},{4,5},{5,6},{6,7},{7,8},{8,9},{9,10},{10,1... | collective-permute-start | bytes 147464 | tf_op jit(solution)/shard_map/ppermute | solution.py:22
  58.7 12.8 %collective-permute-start.12 = (f32[2,1,24,256]{3,2,1,0:T(8,128)S(1)}, f32[2,1,24,256]{3,2,1,0:T(8,128)S(1)}, u32[]{:S(2)}, u32[]{:S(2)}) collective-permute-start(f32[2,1,24,256]{3,2,1,0:T(8,128)S(1)} %get-tuple-element.20), channel_id=1, source_target_pairs={{1,0},{2,1},{3,2},{4,3},{5,4},{6,5},{7,6},{8,7},{9,8},{10,9},{11,1... | collective-permute-start | bytes 147464 | tf_op jit(solution)/shard_map/ppermute | solution.py:23
  67.2 4.6 %collective-permute-start.15 = (f32[2,24,1,256]{3,2,1,0:T(1,128)S(1)}, f32[2,24,1,256]{3,2,1,0:T(1,128)S(1)}, u32[]{:S(2)}, u32[]{:S(2)}) collective-permute-start(f32[2,24,1,256]{3,2,1,0:T(1,128)S(1)} %get-tuple-element.21), channel_id=1, source_target_pairs={{0,64},{1,65},{2,66},{3,67},{4,68},{5,69},{6,70},{7,71},{8,72},{9,... | collective-permute-start | bytes 147464 | tf_op jit(solution)/shard_map/ppermute | solution.py:22
  68.5 3.9 %collective-permute-start.14 = (f32[2,24,1,256]{3,2,1,0:T(1,128)S(1)}, f32[2,24,1,256]{3,2,1,0:T(1,128)S(1)}, u32[]{:S(2)}, u32[]{:S(2)}) collective-permute-start(f32[2,24,1,256]{3,2,1,0:T(1,128)S(1)} %get-tuple-element.22), channel_id=1, source_target_pairs={{64,0},{65,1},{66,2},{67,3},{68,4},{69,5},{70,6},{71,7},{72,8},{73... | collective-permute-start | bytes 147464 | tf_op jit(solution)/shard_map/ppermute | solution.py:23
  71.8 1.0 copy-start.9
  73.2 9.5 %collective-permute-start.16 = (bf16[2,2,24,256]{3,2,1,0:T(8,128)(2,1)S(1)}, bf16[2,2,24,256]{3,2,1,0:T(8,128)(2,1)S(1)}, u32[]{:S(2)}, u32[]{:S(2)}) collective-permute-start(bf16[2,2,24,256]{3,2,1,0:T(8,128)(2,1)S(1)} %get-tuple-element.39), channel_id=1, source_target_pairs={{0,1},{1,2},{2,3},{3,4},{4,5},{5,6},{6,7},{7,8},{8,9},{9,10},{10,1... | collective-permute-start | bytes 147464 | tf_op jit(solution)/shard_map/ppermute | solution.py:22
  75.1 8.7 %collective-permute-start.17 = (bf16[2,2,24,256]{3,2,1,0:T(8,128)(2,1)S(1)}, bf16[2,2,24,256]{3,2,1,0:T(8,128)(2,1)S(1)}, u32[]{:S(2)}, u32[]{:S(2)}) collective-permute-start(bf16[2,2,24,256]{3,2,1,0:T(8,128)(2,1)S(1)} %get-tuple-element.40), channel_id=1, source_target_pairs={{1,0},{2,1},{3,2},{4,3},{5,4},{6,5},{7,6},{8,7},{9,8},{10,9},{11,1... | collective-permute-start | bytes 147464 | tf_op jit(solution)/shard_map/ppermute | solution.py:23
  83.9 4.7 %collective-permute-start.18 = (bf16[2,28,2,256]{3,2,1,0:T(2,128)(2,1)S(1)}, bf16[2,28,2,256]{3,2,1,0:T(2,128)(2,1)S(1)}, u32[]{:S(2)}, u32[]{:S(2)}) collective-permute-start(bf16[2,28,2,256]{3,2,1,0:T(2,128)(2,1)S(1)} %get-tuple-element.31), channel_id=1, source_target_pairs={{0,64},{1,65},{2,66},{3,67},{4,68},{5,69},{6,70},{7,71},{8,72},{9,... | collective-permute-start | bytes 172040 | tf_op jit(solution)/shard_map/ppermute | solution.py:22
  85.2 4.3 %collective-permute-start.19 = (bf16[2,28,2,256]{3,2,1,0:T(2,128)(2,1)S(1)}, bf16[2,28,2,256]{3,2,1,0:T(2,128)(2,1)S(1)}, u32[]{:S(2)}, u32[]{:S(2)}) collective-permute-start(bf16[2,28,2,256]{3,2,1,0:T(2,128)(2,1)S(1)} %get-tuple-element.32), channel_id=1, source_target_pairs={{64,0},{65,1},{66,2},{67,3},{68,4},{69,5},{70,6},{71,7},{72,8},{73... | collective-permute-start | bytes 172040 | tf_op jit(solution)/shard_map/ppermute | solution.py:23
  91.9 15.4 %copy-start.1 = (f32[2,256,576]{1,2,0:T(8,128)}, f32[2,256,576]{1,2,0:T(8,128)S(1)}, u32[]{:S(2)}) copy-start(f32[2,256,576]{1,2,0:T(8,128)S(1)} %fusion.4) | copy-start | bytes 3538948
  91.9 14.5 %collective-permute-start.21 = (f32[2,1,24,256]{3,2,1,0:T(8,128)S(1)}, f32[2,1,24,256]{3,2,1,0:T(8,128)S(1)}, u32[]{:S(2)}, u32[]{:S(2)}) collective-permute-start(f32[2,1,24,256]{3,2,1,0:T(8,128)S(1)} %get-tuple-element.15), channel_id=1, source_target_pairs={{0,1},{1,2},{2,3},{3,4},{4,5},{5,6},{6,7},{7,8},{8,9},{9,10},{10,1... | collective-permute-start | bytes 147464 | tf_op jit(solution)/shard_map/ppermute | solution.py:22
  93.9 12.6 %collective-permute-start.20 = (f32[2,1,24,256]{3,2,1,0:T(8,128)S(1)}, f32[2,1,24,256]{3,2,1,0:T(8,128)S(1)}, u32[]{:S(2)}, u32[]{:S(2)}) collective-permute-start(f32[2,1,24,256]{3,2,1,0:T(8,128)S(1)} %get-tuple-element.16), channel_id=1, source_target_pairs={{1,0},{2,1},{3,2},{4,3},{5,4},{6,5},{7,6},{8,7},{9,8},{10,9},{11,1... | collective-permute-start | bytes 147464 | tf_op jit(solution)/shard_map/ppermute | solution.py:23
  102.1 4.6 %collective-permute-start.23 = (f32[2,24,1,256]{3,2,1,0:T(1,128)S(1)}, f32[2,24,1,256]{3,2,1,0:T(1,128)S(1)}, u32[]{:S(2)}, u32[]{:S(2)}) collective-permute-start(f32[2,24,1,256]{3,2,1,0:T(1,128)S(1)} %get-tuple-element.17), channel_id=1, source_target_pairs={{0,64},{1,65},{2,66},{3,67},{4,68},{5,69},{6,70},{7,71},{8,72},{9,... | collective-permute-start | bytes 147464 | tf_op jit(solution)/shard_map/ppermute | solution.py:22
  103.4 3.9 %collective-permute-start.22 = (f32[2,24,1,256]{3,2,1,0:T(1,128)S(1)}, f32[2,24,1,256]{3,2,1,0:T(1,128)S(1)}, u32[]{:S(2)}, u32[]{:S(2)}) collective-permute-start(f32[2,24,1,256]{3,2,1,0:T(1,128)S(1)} %get-tuple-element.18), channel_id=1, source_target_pairs={{64,0},{65,1},{66,2},{67,3},{68,4},{69,5},{70,6},{71,7},{72,8},{73... | collective-permute-start | bytes 147464 | tf_op jit(solution)/shard_map/ppermute | solution.py:23
  109.1 9.5 %collective-permute-start.24 = (bf16[2,2,24,256]{3,2,1,0:T(8,128)(2,1)S(1)}, bf16[2,2,24,256]{3,2,1,0:T(8,128)(2,1)S(1)}, u32[]{:S(2)}, u32[]{:S(2)}) collective-permute-start(bf16[2,2,24,256]{3,2,1,0:T(8,128)(2,1)S(1)} %get-tuple-element.37), channel_id=1, source_target_pairs={{0,1},{1,2},{2,3},{3,4},{4,5},{5,6},{6,7},{7,8},{8,9},{9,10},{10,1... | collective-permute-start | bytes 147464 | tf_op jit(solution)/shard_map/ppermute | solution.py:22
  111.1 8.7 %collective-permute-start.25 = (bf16[2,2,24,256]{3,2,1,0:T(8,128)(2,1)S(1)}, bf16[2,2,24,256]{3,2,1,0:T(8,128)(2,1)S(1)}, u32[]{:S(2)}, u32[]{:S(2)}) collective-permute-start(bf16[2,2,24,256]{3,2,1,0:T(8,128)(2,1)S(1)} %get-tuple-element.38), channel_id=1, source_target_pairs={{1,0},{2,1},{3,2},{4,3},{5,4},{6,5},{7,6},{8,7},{9,8},{10,9},{11,1... | collective-permute-start | bytes 147464 | tf_op jit(solution)/shard_map/ppermute | solution.py:23
  119.9 4.9 %collective-permute-start.26 = (bf16[2,28,2,256]{3,2,1,0:T(2,128)(2,1)S(1)}, bf16[2,28,2,256]{3,2,1,0:T(2,128)(2,1)S(1)}, u32[]{:S(2)}, u32[]{:S(2)}) collective-permute-start(bf16[2,28,2,256]{3,2,1,0:T(2,128)(2,1)S(1)} %get-tuple-element.29), channel_id=1, source_target_pairs={{0,64},{1,65},{2,66},{3,67},{4,68},{5,69},{6,70},{7,71},{8,72},{9,... | collective-permute-start | bytes 172040 | tf_op jit(solution)/shard_map/ppermute | solution.py:22
  121.2 4.3 %collective-permute-start.27 = (bf16[2,28,2,256]{3,2,1,0:T(2,128)(2,1)S(1)}, bf16[2,28,2,256]{3,2,1,0:T(2,128)(2,1)S(1)}, u32[]{:S(2)}, u32[]{:S(2)}) collective-permute-start(bf16[2,28,2,256]{3,2,1,0:T(2,128)(2,1)S(1)} %get-tuple-element.30), channel_id=1, source_target_pairs={{64,0},{65,1},{66,2},{67,3},{68,4},{69,5},{70,6},{71,7},{72,8},{73... | collective-permute-start | bytes 172040 | tf_op jit(solution)/shard_map/ppermute | solution.py:23
  131.2 15.4 %copy-start.3 = (f32[2,256,576]{1,2,0:T(8,128)}, f32[2,256,576]{1,2,0:T(8,128)S(1)}, u32[]{:S(2)}) copy-start(f32[2,256,576]{1,2,0:T(8,128)S(1)} %fusion.2) | copy-start | bytes 3538948
  131.2 14.5 %collective-permute-start.29 = (f32[2,1,24,256]{3,2,1,0:T(8,128)S(1)}, f32[2,1,24,256]{3,2,1,0:T(8,128)S(1)}, u32[]{:S(2)}, u32[]{:S(2)}) collective-permute-start(f32[2,1,24,256]{3,2,1,0:T(8,128)S(1)} %get-tuple-element.11), channel_id=1, source_target_pairs={{0,1},{1,2},{2,3},{3,4},{4,5},{5,6},{6,7},{7,8},{8,9},{9,10},{10,1... | collective-permute-start | bytes 147464 | tf_op jit(solution)/shard_map/ppermute | solution.py:22
  133.1 12.6 %collective-permute-start.28 = (f32[2,1,24,256]{3,2,1,0:T(8,128)S(1)}, f32[2,1,24,256]{3,2,1,0:T(8,128)S(1)}, u32[]{:S(2)}, u32[]{:S(2)}) collective-permute-start(f32[2,1,24,256]{3,2,1,0:T(8,128)S(1)} %get-tuple-element.12), channel_id=1, source_target_pairs={{1,0},{2,1},{3,2},{4,3},{5,4},{6,5},{7,6},{8,7},{9,8},{10,9},{11,1... | collective-permute-start | bytes 147464 | tf_op jit(solution)/shard_map/ppermute | solution.py:23
  141.4 4.6 %collective-permute-start.31 = (f32[2,24,1,256]{3,2,1,0:T(1,128)S(1)}, f32[2,24,1,256]{3,2,1,0:T(1,128)S(1)}, u32[]{:S(2)}, u32[]{:S(2)}) collective-permute-start(f32[2,24,1,256]{3,2,1,0:T(1,128)S(1)} %get-tuple-element.13), channel_id=1, source_target_pairs={{0,64},{1,65},{2,66},{3,67},{4,68},{5,69},{6,70},{7,71},{8,72},{9,... | collective-permute-start | bytes 147464 | tf_op jit(solution)/shard_map/ppermute | solution.py:22
  142.7 3.9 %collective-permute-start.30 = (f32[2,24,1,256]{3,2,1,0:T(1,128)S(1)}, f32[2,24,1,256]{3,2,1,0:T(1,128)S(1)}, u32[]{:S(2)}, u32[]{:S(2)}) collective-permute-start(f32[2,24,1,256]{3,2,1,0:T(1,128)S(1)} %get-tuple-element.14), channel_id=1, source_target_pairs={{64,0},{65,1},{66,2},{67,3},{68,4},{69,5},{70,6},{71,7},{72,8},{73... | collective-permute-start | bytes 147464 | tf_op jit(solution)/shard_map/ppermute | solution.py:23
  146.0 1.3 copy-start.7
  147.8 9.5 %collective-permute-start.32 = (bf16[2,2,24,256]{3,2,1,0:T(8,128)(2,1)S(1)}, bf16[2,2,24,256]{3,2,1,0:T(8,128)(2,1)S(1)}, u32[]{:S(2)}, u32[]{:S(2)}) collective-permute-start(bf16[2,2,24,256]{3,2,1,0:T(8,128)(2,1)S(1)} %get-tuple-element.35), channel_id=1, source_target_pairs={{0,1},{1,2},{2,3},{3,4},{4,5},{5,6},{6,7},{7,8},{8,9},{9,10},{10,1... | collective-permute-start | bytes 147464 | tf_op jit(solution)/shard_map/ppermute | solution.py:22
  149.7 8.7 %collective-permute-start.33 = (bf16[2,2,24,256]{3,2,1,0:T(8,128)(2,1)S(1)}, bf16[2,2,24,256]{3,2,1,0:T(8,128)(2,1)S(1)}, u32[]{:S(2)}, u32[]{:S(2)}) collective-permute-start(bf16[2,2,24,256]{3,2,1,0:T(8,128)(2,1)S(1)} %get-tuple-element.36), channel_id=1, source_target_pairs={{1,0},{2,1},{3,2},{4,3},{5,4},{6,5},{7,6},{8,7},{9,8},{10,9},{11,1... | collective-permute-start | bytes 147464 | tf_op jit(solution)/shard_map/ppermute | solution.py:23
  158.6 4.4 %collective-permute-start.34 = (bf16[2,28,2,256]{3,2,1,0:T(2,128)(2,1)S(1)}, bf16[2,28,2,256]{3,2,1,0:T(2,128)(2,1)S(1)}, u32[]{:S(2)}, u32[]{:S(2)}) collective-permute-start(bf16[2,28,2,256]{3,2,1,0:T(2,128)(2,1)S(1)} %get-tuple-element.27), channel_id=1, source_target_pairs={{0,64},{1,65},{2,66},{3,67},{4,68},{5,69},{6,70},{7,71},{8,72},{9,... | collective-permute-start | bytes 172040 | tf_op jit(solution)/shard_map/ppermute | solution.py:22
  159.9 4.0 %collective-permute-start.35 = (bf16[2,28,2,256]{3,2,1,0:T(2,128)(2,1)S(1)}, bf16[2,28,2,256]{3,2,1,0:T(2,128)(2,1)S(1)}, u32[]{:S(2)}, u32[]{:S(2)}) collective-permute-start(bf16[2,28,2,256]{3,2,1,0:T(2,128)(2,1)S(1)} %get-tuple-element.28), channel_id=1, source_target_pairs={{64,0},{65,1},{66,2},{67,3},{68,4},{69,5},{70,6},{71,7},{72,8},{73... | collective-permute-start | bytes 172040 | tf_op jit(solution)/shard_map/ppermute | solution.py:23
  167.4 2.3 %copy-start.2 = (f32[2,256,576]{1,2,0:T(8,128)S(1)}, f32[2,256,576]{1,2,0:T(8,128)}, u32[]{:S(2)}) copy-start(f32[2,256,576]{1,2,0:T(8,128)} %copy-done.1) | copy-start | bytes 3538948
  167.4 2.3 %copy-start.4 = (f32[2,256,576]{1,2,0:T(8,128)S(1)}, f32[2,256,576]{1,2,0:T(8,128)}, u32[]{:S(2)}) copy-start(f32[2,256,576]{1,2,0:T(8,128)} %copy-done.3) | copy-start | bytes 3538948
  167.4 2.3 %copy-start.6 = (f32[2,24,24,256]{3,2,1,0:T(8,128)S(1)}, f32[2,24,24,256]{3,2,1,0:T(8,128)}, u32[]{:S(2)}) copy-start(f32[2,24,24,256]{3,2,1,0:T(8,128)} %param.6) | copy-start | bytes 3538948
where the time goes:
time: 174 us; the launch traced here: 171 us
  starting transfers between devices  127 us (73%)
  other arithmetic  16.2 us (9%)
  local copies, waits for them, and re-layouts  11.1 us (6%)
  waiting for transfers between devices  9.9 us (6%)
  matrix products  6.43 us (4%)
    ppermute x16, starting transfers between devices, grow_halo(): from_above = lax.ppermute(low_edge, axis_name, down_perm(axis_size))  88.4 us
    ppermute x16, starting transfers between devices, grow_halo(): from_below = lax.ppermute(high_edge, axis_name, up_perm(axis_size))  25.7 us
    ppermute x16, waiting for transfers between devices, grow_halo(): from_above = lax.ppermute(low_edge, axis_name, down_perm(axis_size))  9.72 us
    ppermute x2, starting transfers between devices, edge_faces(): from_above = lax.ppermute(low_edge, axis_name, down_perm(axis_size))  9.52 us
    dot_general x4, matrix products, local_sweeps(): jnp.einsum('sqe,sek->sqk', solve_mat, window.reshape(num_sys, ext_size *...  6.43 us
    concatenate x4, other arithmetic, grow_halo(): return jnp.concatenate([from_below, values, from_above], axis=grid_dim)  4.14 us
    reshape x2, local copies, waits for them, and re-layouts, local_sweeps(): window.reshape(num_sys, ext_size * ext_size, num_rhs)  4.12 us
  transfers between devices with their start and end apart: 36, of which 12 were waited for; matrix products, arithmetic and copies ran while one was open for 5% of the time, Pallas kernels for 0%

commit v1 on v0

v1 whole, which is shorter than its diff:
```python
import functools

import jax
import jax.numpy as jnp
from jax import lax
from jax.experimental import pallas as pl
from jax.experimental.pallas import tpu as pltpu
from jax.sharding import PartitionSpec as P

SWEEPS = 4
SUB = 24
MARGIN = 2
EXT = SUB + 2 * MARGIN
BAND = 2 * SUB
EDGE = 3
WIN = EXT * BAND
WIN_PAD = 1408
LANES = 128
F32 = jnp.float32
BF16 = jnp.bfloat16
MESH = pl.DeviceIdType.MESH

EDGE_ROWS = tuple(range(EDGE)) + tuple(range(SUB - EDGE, SUB))
INNER_ROWS = tuple(range(EDGE, SUB - EDGE))


def kernel(rows, halves, f_hbm, u_hbm, c_hbm, s_hbm, om_ref, out_hbm, res, cor, app, s_raw, s_edge, s_inner, win, c_raw, c_nbr, c_wide,
           face_x, face_lo, face_hi, diag, send_f, send_b, recv_f, recv_b, loc_sem, side_send, side_recv, csend, crecv, fsend, frecv,
           bsend, brecv):
    core = lax.axis_index("col")
    row = lax.axis_index("row")
    other = 1 - core
    width = 2 * LANES // halves
    has = (row > 0, row < rows - 1)
    near = (row - 1, row + 1)

    mine = pl.multiple_of(core * SUB, 8)
    loads = [
        pltpu.make_async_copy(c_hbm.at[core], c_raw.at[core], loc_sem.at[0]),
        pltpu.make_async_copy(f_hbm.at[core], res.at[:, pl.ds(mine, SUB), :], loc_sem.at[1]),
        pltpu.make_async_copy(u_hbm.at[core], cor.at[:, pl.ds(mine, SUB), :], loc_sem.at[2]),
        pltpu.make_async_copy(s_hbm.at[core], s_raw.at[core], loc_sem.at[3]),
    ]
    for load in loads:
        load.start()

    barrier = pltpu.get_barrier_semaphore()
    pl.semaphore_signal(barrier, inc=1, device_id={"col": other}, device_id_type=MESH)
    for way in range(2):
        @pl.when(has[way])
        def _():
            pl.semaphore_signal(barrier, inc=1, device_id={"row": near[way]}, device_id_type=MESH)
    pl.semaphore_wait(barrier, 1 + has[0].astype(jnp.int32) + has[1].astype(jnp.int32))

    def swap(src, dst, index):
        return pltpu.make_async_remote_copy(src, dst, side_send.at[index], side_recv.at[index], device_id={"col": other}, device_id_type=MESH)

    swaps = [
        swap(c_hbm.at[other], c_raw.at[core], 0),
        swap(f_hbm.at[other], res.at[:, pl.ds(mine, SUB), :], 1),
        swap(u_hbm.at[other], cor.at[:, pl.ds(mine, SUB), :], 2),
        swap(s_hbm.at[other], s_raw.at[core], 3),
    ]
    for item in swaps:
        item.start()

    win[WIN:, :] = jnp.zeros((WIN_PAD - WIN, 2 * LANES), BF16)
    for way in range(2):
        @pl.when(jnp.logical_not(has[way]))
        def _():
            for rnd in range(SWEEPS):
                recv_f[rnd, way] = jnp.zeros(recv_f.shape[2:], F32)
                recv_b[rnd, way] = jnp.zeros(recv_b.shape[2:], BF16)

    loads[0].wait()
    swaps[0].wait()
    for way in range(2):
        @pl.when(has[way])
        def _():
            pltpu.make_async_remote_copy(c_raw, c_nbr.at[1 - way], csend.at[way], crecv.at[1 - way], device_id={"row": near[way]}, device_id_type=MESH).start()

    eye = lax.broadcasted_iota(jnp.int32, (SUB, SUB), 0) == lax.broadcasted_iota(jnp.int32, (SUB, SUB), 1)

    def column(ref, block, x):
        line = jnp.broadcast_to(ref[block, pl.ds(x, 1), :], (SUB, SUB))
        return jnp.broadcast_to(jnp.sum(jnp.where(eye, line, 0.0), axis=1, keepdims=True), (SUB, LANES))

    for x in range(SUB):
        for block in range(2):
            c_wide[x, SUB * block:SUB * (block + 1), :] = column(c_raw, block, x)
    cell = lax.broadcasted_iota(jnp.int32, (BAND, LANES), 0)
    for x in range(SUB):
        own = c_wide[x]
        below = pltpu.roll(own, 1, 0)
        above = pltpu.roll(own, BAND - 1, 0)
        lo = 0.5 * (own + below)
        hi = 0.5 * (own + above)
        total = jnp.where(cell == 0, own, lo) + jnp.where(cell == BAND - 1, own, hi)
        face_lo[x] = jnp.where(cell == 0, 0.0, lo)
        face_hi[x] = jnp.where(cell == BAND - 1, 0.0, hi)
        if x > 0:
            low_x = 0.5 * (c_wide[x - 1] + own)
            face_x[x] = low_x
            total = total + low_x
        if x < SUB - 1:
            total = total + 0.5 * (own + c_wide[x + 1])
        diag[x] = total

    def lanes_of(half):
        return [slice(half * width + LANES * i, half * width + LANES * (i + 1)) for i in range(width // LANES)]

    def neighbourless(x, lanes, last_static=None):
        here = cor[x, :, lanes]
        flux = diag[x] * here - face_lo[x] * pltpu.roll(here, 1, 0) - face_hi[x] * pltpu.roll(here, BAND - 1, 0)
        if last_static is None or x > 0:
            flux = flux - face_x[x] * cor[x - 1, :, lanes]
        if last_static is None or x < SUB - 1:
            flux = flux - face_x[x + 1] * cor[x + 1, :, lanes]
        return flux

    edge_row = (0, SUB - 1)
    second_row = (1, SUB - 2)

    def message(rnd, way, half):
        lane = pl.ds(half * width, width)
        return (
            pltpu.make_async_remote_copy(send_f.at[rnd, way, :, :, lane], recv_f.at[rnd, 1 - way, :, :, lane], fsend.at[rnd, way, half],
                                         frecv.at[rnd, 1 - way, half], device_id={"row": near[way]}, device_id_type=MESH),
            pltpu.make_async_remote_copy(send_b.at[rnd, way, :, lane], recv_b.at[rnd, 1 - way, :, lane], bsend.at[rnd, way, half],
                                         brecv.at[rnd, 1 - way, half], device_id={"row": near[way]}, device_id_type=MESH),
        )

    def send_edges(rnd, half, omega):
        for way in range(2):
            x, y = edge_row[way], second_row[way]
            for lanes in lanes_of(half):
                first = res[x, :, lanes] - omega * neighbourless(x, lanes, True)
                second = res[y, :, lanes] - omega * neighbourless(y, lanes, True)
                res[x, :, lanes] = first
                res[y, :, lanes] = second
                send_f[rnd, way, 0, :, lanes] = cor[x, :, lanes]
                send_f[rnd, way, 1, :, lanes] = first
                send_b[rnd, way, :, lanes] = second.astype(BF16)

            @pl.when(has[way])
            def _():
                for copy in message(rnd, way, half):
                    copy.start()

    def inner_update(rnd, half, omega):
        def body(x, carry):
            for lanes in lanes_of(half):
                new = res[x, :, lanes] - omega * neighbourless(x, lanes)
                res[x, :, lanes] = new
                win[pl.ds(pl.multiple_of((x + MARGIN) * BAND, 16), BAND), lanes] = new.astype(BF16)
            return carry
        lax.fori_loop(2, SUB - 2, body, 0)
        for x in second_row:
            for lanes in lanes_of(half):
                win[(x + MARGIN) * BAND:(x + MARGIN + 1) * BAND, lanes] = res[x, :, lanes].astype(BF16)

    def take_edges(rnd, half, omega):
        for way in range(2):
            @pl.when(has[way])
            def _():
                for copy in message(rnd, 1 - way, half):
                    copy.wait_recv()
        for way in range(2):
            x = edge_row[way]
            face = face_x[0] if way == 0 else face_x[SUB]
            outer, beyond = (1, 0) if way == 0 else (EXT - 2, EXT - 1)
            for lanes in lanes_of(half):
                flux = omega * face * (cor[x, :, lanes] - recv_f[rnd, way, 0, :, lanes])
                new = res[x, :, lanes] - flux
                res[x, :, lanes] = new
                win[(x + MARGIN) * BAND:(x + MARGIN + 1) * BAND, lanes] = new.astype(BF16)
                win[outer * BAND:(outer + 1) * BAND, lanes] = (recv_f[rnd, way, 1, :, lanes] + flux).astype(BF16)
                win[beyond * BAND:(beyond + 1) * BAND, lanes] = recv_b[rnd, way, :, lanes]

    def solve(mat, which, half):
        count = len(which) * SUB
        for block in range(2):
            part = jnp.dot(mat[block], win[:, half * width:(half + 1) * width], preferred_element_type=F32)
            for i, x in enumerate(which):
                cor[x, SUB * block:SUB * (block + 1), half * width:(half + 1) * width] = part[SUB * i:SUB * (i + 1)]

    for item in loads[1:3]:
        item.wait()
    for item in swaps[1:3]:
        item.wait()
    for half in range(halves):
        send_edges(0, half, 1.0)
    for half in range(halves):
        inner_update(0, half, 1.0)

    def keep(x, carry):
        app[x] = cor[x]
        return carry
    lax.fori_loop(0, SUB, keep, 0)

    loads[3].wait()
    swaps[3].wait()
    for chunk in range(0, WIN_PAD, 256):
        size = min(256, WIN_PAD - chunk)
        first = (chunk // BAND) * EXT // 16 * 16
        last = min(EXT * EXT, -(-min(EXT, (chunk + size - 1) // BAND + 1) * EXT // 16) * 16)
        source = lax.broadcasted_iota(jnp.int32, (last - first, size), 0) + first
        target = lax.broadcasted_iota(jnp.int32, (last - first, size), 1) + chunk
        ext_x = lax.shift_right_logical(source * 2341, 16)
        ext_y = source - EXT * ext_x
        for block in range(2):
            band_y = ext_y + (SUB * block - MARGIN)
            hit = (target == ext_x * BAND + band_y) & (band_y >= 0) & (band_y < BAND)
            pick = jnp.where(hit, 1.0, 0.0).astype(BF16)
            moved = lax.dot_general(s_raw[block, first:last, :], pick, (((0,), (0,)), ((), ())), preferred_element_type=F32)
            cut = EDGE * SUB
            s_edge[block, :, chunk:chunk + size] = jnp.concatenate([moved[:cut], moved[-cut:]], axis=0).astype(BF16)
            s_inner[block, :, chunk:chunk + size] = moved[cut:-cut].astype(BF16)

    for way in range(2):
        @pl.when(has[way])
        def _():
            pltpu.make_async_remote_copy(c_raw, c_nbr.at[way], csend.at[1 - way], crecv.at[way], device_id={"row": near[way]}, device_id_type=MESH).wait_recv()
        x = edge_row[way]
        at = 0 if way == 0 else SUB
        for block in range(2):
            part = slice(SUB * block, SUB * (block + 1))
            own = c_wide[x, part]
            beyond = jnp.where(has[way], column(c_nbr.at[way], block, edge_row[1 - way]), own)
            face_x[at, part] = 0.5 * (own + beyond)

    omega = om_ref[core]
    for sweep in range(SWEEPS):
        before = 1.0 if sweep == 0 else omega
        for half in range(halves):
            take_edges(sweep, half, before)
            solve(s_edge, EDGE_ROWS, half)
            if sweep < SWEEPS - 1:
                send_edges(sweep + 1, half, omega)
            solve(s_inner, INNER_ROWS, half)

            def advance(x, carry):
                for lanes in lanes_of(half):
                    app[x, :, lanes] = app[x, :, lanes] + omega * cor[x, :, lanes]
                return carry
            lax.fori_loop(0, SUB, advance, 0)
            if sweep < SWEEPS - 1:
                inner_update(sweep + 1, half, omega)

    theirs = pl.multiple_of(other * SUB, 8)
    back = pltpu.make_async_remote_copy(app.at[:, pl.ds(theirs, SUB), :], out_hbm.at[core], side_send.at[4], side_recv.at[4], device_id={"col": other}, device_id_type=MESH)
    back.start()
    keep_own = pltpu.make_async_copy(app.at[:, pl.ds(mine, SUB), :], out_hbm.at[core], loc_sem.at[4])
    keep_own.start()
    keep_own.wait()
    back.wait()
    for way in range(2):
        @pl.when(has[way])
        def _():
            pltpu.make_async_remote_copy(c_raw, c_nbr.at[1 - way], csend.at[way], crecv.at[1 - way], device_id={"row": near[way]}, device_id_type=MESH).wait_send()
            for rnd in range(SWEEPS):
                for half in range(halves):
                    for copy in message(rnd, way, half):
                        copy.wait_send()


def solution(mesh):
    rows = mesh.shape["row"]
    halves = 2
    grid_spec = P(None, "row", "col", None)

    def local_sweeps(forcing, init_guess, cell_coef, solve_rows, relax_factor):
        systems, _, _, rhs = forcing.shape
        solve_mat = jnp.swapaxes(solve_rows.reshape(systems, SUB * SUB, EXT * EXT), 1, 2)
        any_space = pl.BlockSpec(memory_space=pl.ANY)
        inner = SUB * len(INNER_ROWS)
        edge = SUB * len(EDGE_ROWS)
        return pl.pallas_call(
            functools.partial(kernel, rows, halves),
            out_shape=jax.ShapeDtypeStruct(forcing.shape, F32),
            in_specs=[any_space] * 4 + [pl.BlockSpec(memory_space=pltpu.SMEM)],
            out_specs=any_space,
            scratch_shapes=[
                pltpu.VMEM((SUB, BAND, rhs), F32),
                pltpu.VMEM((SUB, BAND, rhs), F32),
                pltpu.VMEM((SUB, BAND, rhs), F32),
                pltpu.VMEM((2, EXT * EXT, SUB * SUB), BF16),
                pltpu.VMEM((2, edge, WIN_PAD), BF16),
                pltpu.VMEM((2, inner, WIN_PAD), BF16),
                pltpu.VMEM((WIN_PAD, rhs), BF16),
                pltpu.VMEM((2, SUB, SUB), F32),
                pltpu.VMEM((2, 2, SUB, SUB), F32),
                pltpu.VMEM((SUB, BAND, LANES), F32),
                pltpu.VMEM((SUB + 1, BAND, LANES), F32),
                pltpu.VMEM((SUB, BAND, LANES), F32),
                pltpu.VMEM((SUB, BAND, LANES), F32),
                pltpu.VMEM((SUB, BAND, LANES), F32),
                pltpu.VMEM((SWEEPS, 2, 2, BAND, rhs), F32),
                pltpu.VMEM((SWEEPS, 2, BAND, rhs), BF16),
                pltpu.VMEM((SWEEPS, 2, 2, BAND, rhs), F32),
                pltpu.VMEM((SWEEPS, 2, BAND, rhs), BF16),
                pltpu.SemaphoreType.DMA((5,)),
                pltpu.SemaphoreType.DMA((5,)),
                pltpu.SemaphoreType.DMA((5,)),
                pltpu.SemaphoreType.DMA((2,)),
                pltpu.SemaphoreType.DMA((2,)),
                pltpu.SemaphoreType.DMA((SWEEPS, 2, halves)),
                pltpu.SemaphoreType.DMA((SWEEPS, 2, halves)),
                pltpu.SemaphoreType.DMA((SWEEPS, 2, halves)),
                pltpu.SemaphoreType.DMA((SWEEPS, 2, halves)),
            ],
            compiler_params=pltpu.CompilerParams(collective_id=0, has_side_effects=True, vmem_limit_bytes=60 * 1024 * 1024),
        )(forcing, init_guess, cell_coef, solve_mat, relax_factor)

    return jax.shard_map(local_sweeps, mesh=mesh, in_specs=(grid_spec, grid_spec, P(None, "row", "col"), P(None, "row", "col", None, None), P(None)), out_specs=grid_spec, check_vma=False)
```

time: 174 us -> 40.8 us (0.23); the launches traced: 171 us -> 40.7 us
  starting transfers between devices: 127 us -> 0 us
  Pallas kernels: 0 us -> 38.3 us
  other arithmetic: 16.2 us -> 0 us
  waiting for transfers between devices: 9.9 us -> 0 us
  local copies, waits for them, and re-layouts: 11.1 us -> 2.37 us
  matrix products: 6.43 us -> 0 us
    ppermute x36 -> x0, starting transfers between devices: 127 us -> none  [the longest x16 88.4 us: grow_halo(): from_above = lax.ppermute(low_edge, axis_name, down_perm(axis_size))]
    pallas_call x0 -> x1, Pallas kernels: none -> 38.3 us  [local_sweeps(): pl.pallas_call(functools.partial(kernel, rows, halves), out_shape=jax.Sha...]
    ppermute x36 -> x0, waiting for transfers between devices: 9.9 us -> none  [the longest x16 9.72 us: grow_halo(): from_above = lax.ppermute(low_edge, axis_name, down_perm(axis_size))]
    dot_general x4 -> x0, matrix products: 6.43 us -> none  [local_sweeps(): jnp.einsum('sqe,sek->sqk', solve_mat, window.reshape(num_sys, ext_size *...]
    mul x10 -> x0, other arithmetic: 5.91 us -> none  [the longest x4 2.79 us: apply_local(): flux_x = face_x[..., None] * (wide_x[:, 1:] - wide_x[:, :-1])]
    concatenate x4 -> x0, other arithmetic: 4.14 us -> none  [grow_halo(): return jnp.concatenate([from_below, values, from_above], axis=grid_dim)]
    reshape x2 -> x0, local copies, waits for them, and re-layouts: 4.12 us -> none  [local_sweeps(): window.reshape(num_sys, ext_size * ext_size, num_rhs)]
    slice x14 -> x0, local copies, waits for them, and re-layouts: 4.05 us -> none  [the longest x12 2.3 us: grow_halo(): lax.slice_in_dim(values, extent - halo_width, extent, axis=grid_dim)]
  transfers between devices with their start and end apart: 36 -> 0, of which waited for: 12 -> 0; matrix products, arithmetic and copies ran while one was open for 5% -> 0% of each run, Pallas kernels for 0% -> 0%
where the time goes in v1:
time: 40.8 us; the launch traced here: 40.7 us
  Pallas kernels  38.3 us (94%)
  local copies, waits for them, and re-layouts  2.37 us (6%)
    pallas_call x1, Pallas kernels, local_sweeps(): pl.pallas_call(functools.partial(kernel, rows, halves), out_shape=jax.Sha...  38.3 us
    unnamed x1, local copies, waits for them, and re-layouts  2.37 us

profile of v1, /device:TPU:97, one launch (start us, length us, event | category | flops | bytes accessed | tf_op | source)
XLA Modules:
  0.0 40.7 jit_solution(2112448427927241841)
XLA Ops:
  0.0 38.3 %shard_map.55 = f32[2,24,24,256]{3,2,1,0:T(8,128)} custom-call(f32[2,24,24,256]{3,2,1,0:T(8,128)} %f_hbm.1, f32[2,24,24,256]{3,2,1,0:T(8,128)} %u_hbm.1, f32[2,24,24]{2,1,0:T(8,128)} %c_hbm.1, bf16[2,784,576]{2,1,0:T(8,128)(2,1)} %bitcast.3, f32[2]{0:T(128)} %om_ref.1), custom_call_target="tpu_custom_call" | custom-call | tf_op jit(solution)/shard_map/pallas_call | solution.py:278
  38.3 2.4 %copy.7 = f32[2,24,24,256]{3,2,1,0:T(8,128)} copy(f32[2,24,24,256]{3,2,1,0:T(8,128)} %shard_map.55) | data formatting | bytes 2359296

commit v2 on v0

v2 whole, which is shorter than its diff:
```python
import functools

import jax
import jax.numpy as jnp
from jax import lax
from jax.experimental import pallas as pl
from jax.experimental.pallas import tpu as pltpu
from jax.sharding import PartitionSpec as P

SWEEPS = 4
SUB = 24
MARGIN = 2
EXT = SUB + 2 * MARGIN
BAND = 2 * SUB
SLOT = 32
OUTER = 8
INNER = EXT - OUTER
LANES = 128
RHS = 2 * LANES
HALVES = 2
F32 = jnp.float32
BF16 = jnp.bfloat16
MESH = pl.DeviceIdType.MESH

EDGE_ROWS = (0, 1, 2, SUB - 3, SUB - 2, SUB - 1)
ROW_ORDER = EDGE_ROWS + tuple(range(3, SUB - 3))
EDGE_CELLS = SUB * len(EDGE_ROWS)
CELLS = SUB * SUB
CHUNK = EDGE_CELLS
EDGE_ROW = (0, SUB - 1)
SECOND_ROW = (1, SUB - 2)
PLACES = ((0, 1, 2, 3), (7, 6, 5, 4))
FIRST = 80


def kernel(rows, f_hbm, u_hbm, c_hbm, s_hbm, om_ref, out_ref, res, cor, app, fin, pre, s_raw, s_out, s_in, w_out, w_in, c_own, c_raw, c_nbr,
           c_wide, c_part, face_x, face_lo, face_hi, cross, diag, u_edge, f_edge, send_0, recv_0, send_f, send_b, recv_f, recv_b,
           loc_sem, edge_sem, side_send, side_recv, csend, crecv, send0_sem, recv0_sem, fsend, frecv, bsend, brecv, back_send, back_recv):
    core = lax.axis_index("col")
    row = lax.axis_index("row")
    other = 1 - core
    sys = lax.rem(core + row, 2)
    systems = (sys, 1 - sys)
    has = (row > 0, row < rows - 1)
    near = (jnp.maximum(row - 1, 0), jnp.minimum(row + 1, rows - 1))
    mine = pl.multiple_of(core * SUB, 8)
    width = RHS // HALVES

    def lanes_of(half):
        return [slice(half * width + LANES * i, half * width + LANES * (i + 1)) for i in range(width // LANES)]

    all_lanes = [slice(LANES * i, LANES * (i + 1)) for i in range(RHS // LANES)]

    load_c = pltpu.make_async_copy(c_hbm, c_own, loc_sem.at[0])
    load_c.start()
    edge_loads = []
    for j in range(2):
        for way in range(2):
            edge_loads.append(pltpu.make_async_copy(u_hbm.at[systems[j], (SUB - 3) * way:(SUB - 3) * way + 3], u_edge.at[j, way], edge_sem.at[j, way, 0]))
            edge_loads.append(pltpu.make_async_copy(f_hbm.at[systems[j], (SUB - 2) * way:(SUB - 2) * way + 2], f_edge.at[j, way], edge_sem.at[j, way, 1]))
    for load in edge_loads:
        load.start()
    load_c_raw = pltpu.make_async_copy(c_hbm.at[sys], c_raw.at[core], loc_sem.at[4])
    load_s = pltpu.make_async_copy(s_hbm.at[sys], s_raw.at[core], loc_sem.at[3])
    load_f = pltpu.make_async_copy(f_hbm.at[sys], res.at[:, pl.ds(mine, SUB), :], loc_sem.at[1])
    load_u = pltpu.make_async_copy(u_hbm.at[sys], cor.at[:, pl.ds(mine, SUB), :], loc_sem.at[2])
    for load in (load_c_raw, load_s, load_f, load_u):
        load.start()

    barrier = pltpu.get_barrier_semaphore()
    for way in range(2):
        @pl.when(has[way])
        def _():
            for col in range(2):
                pl.semaphore_signal(barrier, inc=1, device_id=(col, near[way]), device_id_type=MESH)
    pl.semaphore_signal(barrier, inc=1, device_id={"col": other}, device_id_type=MESH)

    eye = lax.broadcasted_iota(jnp.int32, (SUB, SUB), 0) == lax.broadcasted_iota(jnp.int32, (SUB, SUB), 1)

    def column(ref, lead, x):
        line = jnp.broadcast_to(ref[lead + (pl.ds(x, 1), slice(None))], (SUB, SUB))
        return jnp.broadcast_to(jnp.sum(jnp.where(eye, line, 0.0), axis=1, keepdims=True), (SUB, LANES))

    load_c.wait()
    for j in range(2):
        for x in EDGE_ROWS:
            c_part[j, x] = column(c_own, (systems[j],), x)
    for load in edge_loads:
        load.wait()
    spot = lax.broadcasted_iota(jnp.int32, (SUB, LANES), 0)
    for j in range(2):
        for way in range(2):
            step = 1 if way == 0 else -1
            place = (0, 1, 2) if way == 0 else (2, 1, 0)
            into = (0, 1) if way == 0 else (1, 0)
            at = [EDGE_ROW[way] + step * i for i in range(3)]
            c = [c_part[j, x] for x in at]
            link = [0.5 * (c[0] + c[1]), 0.5 * (c[1] + c[2])]
            for i in range(2):
                lo = jnp.where(spot == 0, 0.0, 0.5 * (c[i] + pltpu.roll(c[i], 1, 0)))
                hi = jnp.where(spot == SUB - 1, 0.0, 0.5 * (c[i] + pltpu.roll(c[i], SUB - 1, 0)))
                wall = jnp.where((spot == 0) & (core == 0) | (spot == SUB - 1) & (core == 1), c[i], 0.0)
                total = lo + hi + wall + link[i]
                if i == 1:
                    total = total + link[0]
                for lanes in all_lanes:
                    u = [u_edge[j, way, place[n], :, lanes] for n in range(3)]
                    flux = total * u[i] - lo * pltpu.roll(u[i], 1, 0) - hi * pltpu.roll(u[i], SUB - 1, 0) - link[i] * u[i + 1]
                    if i == 1:
                        flux = flux - link[0] * u[0]
                    send_0[way, j, SUB * (i + 1):SUB * (i + 2), lanes] = f_edge[j, way, into[i], :, lanes] - flux
                    if i == 0:
                        send_0[way, j, 0:SUB, lanes] = u[0]
            tile = jnp.where(core == 0, u_edge[j, way, place[1], SUB - 8:SUB, :], u_edge[j, way, place[1], 0:8, :])
            send_0[way, j, 3 * SUB:FIRST, :] = tile

    source = lax.broadcasted_iota(jnp.int32, (4 * EXT, 4 * SLOT), 0)
    target = lax.broadcasted_iota(jnp.int32, (4 * EXT, 4 * SLOT), 1)
    ext_x = lax.shift_right_logical(source * 2341, 16)
    ext_y = source - EXT * ext_x

    def reorder(block):
        shift = (SUB - (BAND - SLOT)) * block - MARGIN
        inside = ext_y + SUB * block - MARGIN
        hit = (target == ext_x * SLOT + ext_y + shift) & (inside >= 0) & (inside < BAND)
        pick = jnp.where(hit, 1.0, 0.0).astype(BF16)
        groups = EXT // 4
        for group in range(groups):
            moved = lax.dot_general(s_raw[block, 4 * EXT * group:4 * EXT * (group + 1), :], pick, (((0,), (0,)), ((), ())), preferred_element_type=F32)
            cut = 3 * SUB
            moved = jnp.concatenate([moved[:cut], moved[-cut:], moved[cut:-cut]], axis=0).astype(BF16)
            if group == 0:
                s_out[block, :, 0:4 * SLOT] = moved
            elif group == groups - 1:
                s_out[block, :, 4 * SLOT:] = moved
            else:
                s_in[block, :, 4 * SLOT * (group - 1):4 * SLOT * group] = moved

    load_s.wait()
    reorder(core)

    pl.semaphore_wait(barrier, 1 + 2 * has[0].astype(jnp.int32) + 2 * has[1].astype(jnp.int32))

    def start_message(way, j, half):
        lane = pl.ds(half * width, width)
        col = other if j == 0 else core
        return pltpu.make_async_remote_copy(send_0.at[way, j, :, lane], recv_0.at[1 - way, core, :, lane], send0_sem.at[way, j, half],
                                            recv0_sem.at[1 - way, core, half], device_id=(col, near[way]), device_id_type=MESH)

    def coef_message(way, j):
        col = other if j == 0 else core
        return pltpu.make_async_remote_copy(c_own.at[systems[j]], c_nbr.at[1 - way, core], csend.at[way, j], crecv.at[1 - way, core],
                                            device_id=(col, near[way]), device_id_type=MESH)

    for half in range(HALVES):
        for way in range(2):
            @pl.when(has[way])
            def _():
                for j in range(2):
                    start_message(way, j, half).start()
                    if half == 0:
                        coef_message(way, j).start()

    def swap(src, dst, index):
        return pltpu.make_async_remote_copy(src, dst, side_send.at[index], side_recv.at[index], device_id={"col": other}, device_id_type=MESH)

    swaps = [
        swap(c_hbm.at[1 - sys], c_raw.at[core], 0),
        swap(f_hbm.at[1 - sys], res.at[:, pl.ds(mine, SUB), :], 1),
        swap(u_hbm.at[1 - sys], cor.at[:, pl.ds(mine, SUB), :], 2),
        swap(s_hbm.at[1 - sys], s_raw.at[core], 3),
    ]
    for item in swaps:
        item.start()

    for way in range(2):
        @pl.when(jnp.logical_not(has[way]))
        def _():
            recv_0[way] = jnp.zeros(recv_0.shape[1:], F32)
            c_nbr[way] = jnp.zeros(c_nbr.shape[1:], F32)
            for rnd in range(SWEEPS - 1):
                recv_f[rnd, way] = jnp.zeros(recv_f.shape[2:], F32)
                recv_b[rnd, way] = jnp.zeros(recv_b.shape[2:], BF16)

    load_c_raw.wait()
    swaps[0].wait()
    for x in range(SUB):
        for block in range(2):
            c_wide[x, SUB * block:SUB * (block + 1), :] = column(c_raw, (block,), x)
    cell = lax.broadcasted_iota(jnp.int32, (BAND, LANES), 0)
    for x in range(SUB):
        own = c_wide[x]
        lo = 0.5 * (own + pltpu.roll(own, 1, 0))
        hi = 0.5 * (own + pltpu.roll(own, BAND - 1, 0))
        total = jnp.where(cell == 0, own, lo) + jnp.where(cell == BAND - 1, own, hi)
        face_lo[x] = jnp.where(cell == 0, 0.0, lo)
        face_hi[x] = jnp.where(cell == BAND - 1, 0.0, hi)
        if x > 0:
            low_x = 0.5 * (c_wide[x - 1] + own)
            face_x[x] = low_x
            total = total + low_x
        if x < SUB - 1:
            total = total + 0.5 * (own + c_wide[x + 1])
        diag[x] = total

    def neighbourless(x, lanes, static=False):
        here = cor[x, :, lanes]
        flux = diag[x] * here - face_lo[x] * pltpu.roll(here, 1, 0) - face_hi[x] * pltpu.roll(here, BAND - 1, 0)
        if not static or x > 0:
            flux = flux - face_x[x] * cor[x - 1, :, lanes]
        if not static or x < SUB - 1:
            flux = flux - face_x[x + 1] * cor[x + 1, :, lanes]
        return flux

    def put(window, place, lanes, values):
        low = values.astype(BF16)
        at = pl.ds(place * SLOT, SLOT) if isinstance(place, int) else pl.ds(pl.multiple_of(place * SLOT, SLOT), SLOT)
        window[0, at, lanes] = low[0:SLOT]
        window[1, at, lanes] = low[BAND - SLOT:BAND]

    def message(rnd, way, half):
        lane = pl.ds(half * width, width)
        to = (other, near[way])
        return (
            pltpu.make_async_remote_copy(send_f.at[rnd, way, :, :, lane], recv_f.at[rnd, 1 - way, :, :, lane], fsend.at[rnd, way, half],
                                         frecv.at[rnd, 1 - way, half], device_id=to, device_id_type=MESH),
            pltpu.make_async_remote_copy(send_b.at[rnd, way, :, lane], recv_b.at[rnd, 1 - way, :, lane], bsend.at[rnd, way, half],
                                         brecv.at[rnd, 1 - way, half], device_id=to, device_id_type=MESH),
        )

    def update_edges(omega, half, rnd=None):
        for way in range(2):
            x, y = EDGE_ROW[way], SECOND_ROW[way]
            for lanes in lanes_of(half):
                first = res[x, :, lanes] - omega * neighbourless(x, lanes, True)
                second = res[y, :, lanes] - omega * neighbourless(y, lanes, True)
                res[x, :, lanes] = first
                res[y, :, lanes] = second
                if rnd is not None:
                    send_f[rnd, way, 0, :, lanes] = cor[x, :, lanes]
                    send_f[rnd, way, 1, :, lanes] = first
                    send_b[rnd, way, :, lanes] = second.astype(BF16)
            if rnd is not None:
                @pl.when(has[way])
                def _():
                    for copy in message(rnd, way, half):
                        copy.start()

    def update_inner(omega):
        def body(x, carry):
            for lanes in all_lanes:
                new = res[x, :, lanes] - omega * neighbourless(x, lanes)
                res[x, :, lanes] = new
                put(w_in, x - 2, lanes, new)
            return carry
        lax.fori_loop(2, SUB - 2, body, 0)
        for way in range(2):
            for lanes in all_lanes:
                put(w_out, PLACES[way][3], lanes, res[SECOND_ROW[way], :, lanes])

    def presolve():
        for block in range(2):
            for part in range(0, CELLS, CHUNK):
                pre[block, part:part + CHUNK] = jnp.dot(s_in[block, part:part + CHUNK], w_in[block], preferred_element_type=F32)

    def take_edges(rnd, half, omega):
        for way in range(2):
            @pl.when(has[way])
            def _():
                if rnd == 0:
                    for block in range(2):
                        lane = pl.ds(half * width, width)
                        pltpu.make_async_remote_copy(send_0.at[way, block, :, lane], recv_0.at[way, block, :, lane], send0_sem.at[way, block, half],
                                                     recv0_sem.at[way, block, half], device_id=(other, near[way]), device_id_type=MESH).wait_recv()
                else:
                    for copy in message(rnd - 1, 1 - way, half):
                        copy.wait_recv()
        for way in range(2):
            x = EDGE_ROW[way]
            face = face_x[0] if way == 0 else face_x[SUB]
            for lanes in lanes_of(half):
                if rnd == 0:
                    z_far, r_far, r_beyond = [jnp.concatenate([recv_0[way, block, SUB * i:SUB * (i + 1), lanes] for block in range(2)], axis=0) for i in range(3)]
                    none = jnp.zeros((SUB - 8, LANES), F32)
                    z_beyond = jnp.concatenate([none] + [recv_0[way, block, 3 * SUB:FIRST, lanes] for block in range(2)] + [none], axis=0)
                    side = cross[way, 0] * (z_far - pltpu.roll(z_far, 1, 0))
                    r_far = r_far - side + pltpu.roll(side, BAND - 1, 0)
                    side = cross[way, 1] * (z_beyond - pltpu.roll(z_beyond, 1, 0))
                    r_beyond = r_beyond - side + pltpu.roll(side, BAND - 1, 0)
                else:
                    z_far = recv_f[rnd - 1, way, 0, :, lanes]
                    r_far = recv_f[rnd - 1, way, 1, :, lanes]
                    r_beyond = recv_b[rnd - 1, way, :, lanes]
                flux = omega * face * (cor[x, :, lanes] - z_far)
                new = res[x, :, lanes] - flux
                res[x, :, lanes] = new
                put(w_out, PLACES[way][0], lanes, r_beyond)
                put(w_out, PLACES[way][1], lanes, r_far + flux)
                put(w_out, PLACES[way][2], lanes, new)

    def solve(block, part, lanes):
        return pre[block, part:part + CHUNK, lanes] + jnp.dot(s_out[block, part:part + CHUNK], w_out[block, :, lanes], preferred_element_type=F32)

    def rows_of(part):
        return ROW_ORDER[part // SUB:(part + CHUNK) // SUB]

    for load in (load_f, load_u):
        load.wait()
    for item in swaps[1:3]:
        item.wait()
    for half in range(HALVES):
        update_edges(1.0, half)
    update_inner(1.0)
    for block in range(2):
        for x in range(SUB):
            app[block, x] = cor[x, SUB * block:SUB * (block + 1), :]
    swaps[3].wait()
    reorder(other)
    presolve()

    for way in range(2):
        @pl.when(has[way])
        def _():
            for block in range(2):
                pltpu.make_async_remote_copy(c_own.at[block], c_nbr.at[way, block], csend.at[way, block], crecv.at[way, block],
                                             device_id=(other, near[way]), device_id_type=MESH).wait_recv()
        own = c_wide[EDGE_ROW[way]]
        beyond = [jnp.concatenate([column(c_nbr, (way, block), x) for block in range(2)], axis=0) for x in (EDGE_ROW[1 - way], SECOND_ROW[1 - way])]
        face_x[0 if way == 0 else SUB] = 0.5 * (own + jnp.where(has[way], beyond[0], own))
        for i in range(2):
            cross[way, i] = jnp.where(cell == SUB, 0.5 * (beyond[i] + pltpu.roll(beyond[i], 1, 0)), 0.0)

    omega = om_ref[sys]
    for sweep in range(SWEEPS - 1):
        before = 1.0 if sweep == 0 else omega
        for half in range(HALVES):
            lanes = slice(half * width, (half + 1) * width)
            take_edges(sweep, half, before)
            for block in range(2):
                part = solve(block, 0, lanes)
                for i, x in enumerate(EDGE_ROWS):
                    cor[x, SUB * block:SUB * (block + 1), lanes] = part[SUB * i:SUB * (i + 1)]
            update_edges(omega, half, sweep)
        for block in range(2):
            for x in EDGE_ROWS:
                app[block, x] = app[block, x] + omega * cor[x, SUB * block:SUB * (block + 1), :]
            for at in range(EDGE_CELLS, CELLS, CHUNK):
                part = solve(block, at, slice(0, RHS))
                for i, x in enumerate(rows_of(at)):
                    piece = part[SUB * i:SUB * (i + 1)]
                    cor[x, SUB * block:SUB * (block + 1), :] = piece
                    app[block, x] = app[block, x] + omega * piece
        update_inner(omega)
        presolve()

    def back(half):
        lane = pl.ds(half * width, width)
        return pltpu.make_async_remote_copy(fin.at[:, :, lane], out_ref.at[sys, :, :, lane], back_send.at[half], back_recv.at[half],
                                            device_id={"col": other}, device_id_type=MESH)

    for half in range(HALVES):
        lanes = slice(half * width, (half + 1) * width)
        take_edges(SWEEPS - 1, half, omega)
        for at in range(0, CELLS, CHUNK):
            part = solve(other, at, lanes)
            for i, x in enumerate(rows_of(at)):
                fin[x, :, lanes] = app[other, x, :, lanes] + omega * part[SUB * i:SUB * (i + 1)]
        back(half).start()
    for at in range(0, CELLS, CHUNK):
        part = solve(core, at, slice(0, RHS))
        for i, x in enumerate(rows_of(at)):
            out_ref[sys, x] = app[core, x] + omega * part[SUB * i:SUB * (i + 1)]

    for half in range(HALVES):
        back(half).wait_send()
        lane = pl.ds(half * width, width)
        pltpu.make_async_remote_copy(fin.at[:, :, lane], out_ref.at[1 - sys, :, :, lane], back_send.at[half], back_recv.at[half],
                                     device_id={"col": other}, device_id_type=MESH).wait_recv()
    for way in range(2):
        @pl.when(has[way])
        def _():
            for j in range(2):
                coef_message(way, j).wait_send()
            for half in range(HALVES):
                for j in range(2):
                    start_message(way, j, half).wait_send()
                for rnd in range(SWEEPS - 1):
                    for copy in message(rnd, way, half):
                        copy.wait_send()


def solution(mesh):
    rows = mesh.shape["row"]
    grid_spec = P(None, "row", "col", None)

    def local_sweeps(forcing, init_guess, cell_coef, solve_rows, relax_factor):
        solve_mat = jnp.swapaxes(solve_rows.reshape(2, CELLS, EXT * EXT), 1, 2)
        any_space = pl.BlockSpec(memory_space=pl.ANY)
        rounds = SWEEPS - 1
        wide = (SUB, BAND, LANES)
        dma = pltpu.SemaphoreType.DMA
        held = [pltpu.with_memory_space_constraint(v, pltpu.HBM) for v in (forcing, init_guess, cell_coef, solve_mat, relax_factor)]
        return pl.pallas_call(
            functools.partial(kernel, rows),
            out_shape=jax.ShapeDtypeStruct(forcing.shape, F32),
            in_specs=[any_space] * 4 + [pl.BlockSpec(memory_space=pltpu.SMEM)],
            out_specs=pl.BlockSpec(memory_space=pltpu.VMEM),
            scratch_shapes=[
                pltpu.VMEM((SUB, BAND, RHS), F32),
                pltpu.VMEM((SUB, BAND, RHS), F32),
                pltpu.VMEM((2, SUB, SUB, RHS), F32),
                pltpu.VMEM((SUB, SUB, RHS), F32),
                pltpu.VMEM((2, CELLS, RHS), F32),
                pltpu.VMEM((2, EXT * EXT, CELLS), BF16),
                pltpu.VMEM((2, CELLS, OUTER * SLOT), BF16),
                pltpu.VMEM((2, CELLS, INNER * SLOT), BF16),
                pltpu.VMEM((2, OUTER * SLOT, RHS), BF16),
                pltpu.VMEM((2, INNER * SLOT, RHS), BF16),
                pltpu.VMEM((2, SUB, SUB), F32),
                pltpu.VMEM((2, SUB, SUB), F32),
                pltpu.VMEM((2, 2, SUB, SUB), F32),
                pltpu.VMEM(wide, F32),
                pltpu.VMEM((2, SUB, SUB, LANES), F32),
                pltpu.VMEM((SUB + 1, BAND, LANES), F32),
                pltpu.VMEM(wide, F32),
                pltpu.VMEM(wide, F32),
                pltpu.VMEM((2, 2, BAND, LANES), F32),
                pltpu.VMEM(wide, F32),
                pltpu.VMEM((2, 2, 3, SUB, RHS), F32),
                pltpu.VMEM((2, 2, 2, SUB, RHS), F32),
                pltpu.VMEM((2, 2, FIRST, RHS), F32),
                pltpu.VMEM((2, 2, FIRST, RHS), F32),
                pltpu.VMEM((rounds, 2, 2, BAND, RHS), F32),
                pltpu.VMEM((rounds, 2, BAND, RHS), BF16),
                pltpu.VMEM((rounds, 2, 2, BAND, RHS), F32),
                pltpu.VMEM((rounds, 2, BAND, RHS), BF16),
                dma((5,)), dma((2, 2, 2)), dma((4,)), dma((4,)), dma((2, 2)), dma((2, 2)), dma((2, 2, HALVES)), dma((2, 2, HALVES)),
                dma((rounds, 2, HALVES)), dma((rounds, 2, HALVES)), dma((rounds, 2, HALVES)), dma((rounds, 2, HALVES)),
                dma((HALVES,)), dma((HALVES,)),
            ],
            compiler_params=pltpu.CompilerParams(collective_id=0, has_side_effects=True, vmem_limit_bytes=40 * 1024 * 1024),
        )(*held)

    return jax.shard_map(local_sweeps, mesh=mesh, in_specs=(grid_spec, grid_spec, P(None, "row", "col"), P(None, "row", "col", None, None), P(None)), out_specs=grid_spec, check_vma=False)
```

time: 174 us -> 34.9 us (0.20); the launches traced: 171 us -> 34.7 us
  starting transfers between devices: 127 us -> 0 us
  Pallas kernels: 0 us -> 33.7 us
  other arithmetic: 16.2 us -> 0 us
  local copies, waits for them, and re-layouts: 11.1 us -> 1.02 us
  waiting for transfers between devices: 9.9 us -> 0 us
  matrix products: 6.43 us -> 0 us
    ppermute x36 -> x0, starting transfers between devices: 127 us -> none  [the longest x16 88.4 us: grow_halo(): from_above = lax.ppermute(low_edge, axis_name, down_perm(axis_size))]
    pallas_call x0 -> x1, Pallas kernels: none -> 33.7 us  [local_sweeps(): pl.pallas_call(functools.partial(kernel, rows), out_shape=jax.ShapeDtypeS...]
    ppermute x36 -> x0, waiting for transfers between devices: 9.9 us -> none  [the longest x16 9.72 us: grow_halo(): from_above = lax.ppermute(low_edge, axis_name, down_perm(axis_size))]
    dot_general x4 -> x0, matrix products: 6.43 us -> none  [local_sweeps(): jnp.einsum('sqe,sek->sqk', solve_mat, window.reshape(num_sys, ext_size *...]
    mul x10 -> x0, other arithmetic: 5.91 us -> none  [the longest x4 2.79 us: apply_local(): flux_x = face_x[..., None] * (wide_x[:, 1:] - wide_x[:, :-1])]
    concatenate x4 -> x0, other arithmetic: 4.14 us -> none  [grow_halo(): return jnp.concatenate([from_below, values, from_above], axis=grid_dim)]
    reshape x2 -> x0, local copies, waits for them, and re-layouts: 4.12 us -> none  [local_sweeps(): window.reshape(num_sys, ext_size * ext_size, num_rhs)]
    slice x14 -> x0, local copies, waits for them, and re-layouts: 4.05 us -> none  [the longest x12 2.3 us: grow_halo(): lax.slice_in_dim(values, extent - halo_width, extent, axis=grid_dim)]
  transfers between devices with their start and end apart: 36 -> 0, of which waited for: 12 -> 0; matrix products, arithmetic and copies ran while one was open for 5% -> 0% of each run, Pallas kernels for 0% -> 0%
where the time goes in v2:
time: 34.9 us; the launch traced here: 34.7 us
  Pallas kernels  33.7 us (97%)
  local copies, waits for them, and re-layouts  1.02 us (3%)
    pallas_call x1, Pallas kernels, local_sweeps(): pl.pallas_call(functools.partial(kernel, rows), out_shape=jax.ShapeDtypeS...  33.7 us
    unnamed x1, local copies, waits for them, and re-layouts  1.02 us

profile of v2, /device:TPU:97, one launch (start us, length us, event | category | flops | bytes accessed | tf_op | source)
XLA Modules:
  0.0 34.7 jit_solution(7681480022267416200)
XLA Ops:
  0.0 33.7 %shard_map.55 = f32[2,24,24,256]{3,2,1,0:T(8,128)S(1)} custom-call(f32[2,24,24,256]{3,2,1,0:T(8,128)} %f_hbm.1, f32[2,24,24,256]{3,2,1,0:T(8,128)} %u_hbm.1, f32[2,24,24]{2,1,0:T(8,128)} %c_hbm.1, bf16[2,784,576]{2,1,0:T(8,128)(2,1)} %bitcast.3, f32[2]{0:T(128)} %om_ref.1), custom_call_target="tpu_custom_call" | custom-call | tf_op jit(solution)/shard_map/pallas_call | solution.py:403
  33.7 1.0 %copy.7 = f32[2,24,24,256]{3,2,1,0:T(8,128)} copy(f32[2,24,24,256]{3,2,1,0:T(8,128)S(1)} %shard_map.55) | data formatting | bytes 2359296

commit v3 on v2

--- a/solution.py
+++ b/solution.py
@@ -34,8 +34,8 @@
 
 
 def kernel(rows, f_hbm, u_hbm, c_hbm, s_hbm, om_ref, out_ref, res, cor, app, fin, pre, s_raw, s_out, s_in, w_out, w_in, c_own, c_raw, c_nbr,
-           c_wide, c_part, face_x, face_lo, face_hi, cross, diag, u_edge, f_edge, send_0, recv_0, send_f, send_b, recv_f, recv_b,
-           loc_sem, edge_sem, side_send, side_recv, csend, crecv, send0_sem, recv0_sem, fsend, frecv, bsend, brecv, back_send, back_recv):
+           c_wide, c_part, face_x, face_lo, face_hi, cross, diag, u_edge, f_edge, f_swap, u_swap, so_swap, si_swap, w_fin, fin_recv, send_0, recv_0, send_f, send_b, recv_f, recv_b,
+           loc_sem, s_sem, edge_sem, side_send, side_recv, csend, crecv, send0_sem, recv0_sem, zsend, zrecv, fsend, frecv, bsend, brecv, back_send, back_recv):
     core = lax.axis_index("col")
     row = lax.axis_index("row")
     other = 1 - core
@@ -61,10 +61,12 @@
     for load in edge_loads:
         load.start()
     load_c_raw = pltpu.make_async_copy(c_hbm.at[sys], c_raw.at[core], loc_sem.at[4])
-    load_s = pltpu.make_async_copy(s_hbm.at[sys], s_raw.at[core], loc_sem.at[3])
+    load_s = [pltpu.make_async_copy(s_hbm.at[systems[j]], s_raw.at[j], s_sem.at[j]) for j in range(2)]
     load_f = pltpu.make_async_copy(f_hbm.at[sys], res.at[:, pl.ds(mine, SUB), :], loc_sem.at[1])
     load_u = pltpu.make_async_copy(u_hbm.at[sys], cor.at[:, pl.ds(mine, SUB), :], loc_sem.at[2])
-    for load in (load_c_raw, load_s, load_f, load_u):
+    load_f_swap = pltpu.make_async_copy(f_hbm.at[1 - sys], f_swap, loc_sem.at[3])
+    load_u_swap = pltpu.make_async_copy(u_hbm.at[1 - sys], u_swap, loc_sem.at[5])
+    for load in (load_c_raw, load_s[1], load_f_swap, load_u_swap, load_s[0], load_f, load_u):
         load.start()
 
     barrier = pltpu.get_barrier_semaphore()
@@ -119,56 +121,66 @@
     ext_x = lax.shift_right_logical(source * 2341, 16)
     ext_y = source - EXT * ext_x
 
-    def reorder(block):
-        shift = (SUB - (BAND - SLOT)) * block - MARGIN
-        inside = ext_y + SUB * block - MARGIN
-        hit = (target == ext_x * SLOT + ext_y + shift) & (inside >= 0) & (inside < BAND)
-        pick = jnp.where(hit, 1.0, 0.0).astype(BF16)
+    shift = (SUB - (BAND - SLOT)) * core - MARGIN
+    inside = ext_y + SUB * core - MARGIN
+    hit = (target == ext_x * SLOT + ext_y + shift) & (inside >= 0) & (inside < BAND)
+    pick = jnp.where(hit, 1.0, 0.0).astype(BF16)
+
+    def reorder(j, outer, inner):
         groups = EXT // 4
         for group in range(groups):
-            moved = lax.dot_general(s_raw[block, 4 * EXT * group:4 * EXT * (group + 1), :], pick, (((0,), (0,)), ((), ())), preferred_element_type=F32)
+            moved = lax.dot_general(s_raw[j, 4 * EXT * group:4 * EXT * (group + 1), :], pick, (((0,), (0,)), ((), ())), preferred_element_type=F32)
             cut = 3 * SUB
             moved = jnp.concatenate([moved[:cut], moved[-cut:], moved[cut:-cut]], axis=0).astype(BF16)
             if group == 0:
-                s_out[block, :, 0:4 * SLOT] = moved
+                outer[:, 0:4 * SLOT] = moved
             elif group == groups - 1:
-                s_out[block, :, 4 * SLOT:] = moved
+                outer[:, 4 * SLOT:] = moved
             else:
-                s_in[block, :, 4 * SLOT * (group - 1):4 * SLOT * group] = moved
-
-    load_s.wait()
-    reorder(core)
+                inner[:, 4 * SLOT * (group - 1):4 * SLOT * group] = moved
+
+    load_s[1].wait()
+    reorder(1, so_swap, si_swap)
+    load_s[0].wait()
+    reorder(0, s_out.at[core], s_in.at[core])
+    load_f_swap.wait()
+    load_u_swap.wait()
 
     pl.semaphore_wait(barrier, 1 + 2 * has[0].astype(jnp.int32) + 2 * has[1].astype(jnp.int32))
 
-    def start_message(way, j, half):
+    def start_message(way, col, half):
         lane = pl.ds(half * width, width)
-        col = other if j == 0 else core
-        return pltpu.make_async_remote_copy(send_0.at[way, j, :, lane], recv_0.at[1 - way, core, :, lane], send0_sem.at[way, j, half],
+        j = other if col == 0 else core
+        return pltpu.make_async_remote_copy(send_0.at[way, j, :, lane], recv_0.at[1 - way, core, :, lane], send0_sem.at[way, col, half],
                                             recv0_sem.at[1 - way, core, half], device_id=(col, near[way]), device_id_type=MESH)
 
-    def coef_message(way, j):
-        col = other if j == 0 else core
-        return pltpu.make_async_remote_copy(c_own.at[systems[j]], c_nbr.at[1 - way, core], csend.at[way, j], crecv.at[1 - way, core],
+    def coef_message(way, col):
+        there = lax.rem(sys + (other if col == 0 else core), 2)
+        tile = pl.ds((SUB - 8) * way, 8)
+        return pltpu.make_async_remote_copy(c_own.at[there, tile], c_nbr.at[1 - way, core], csend.at[way, col], crecv.at[1 - way, core],
                                             device_id=(col, near[way]), device_id_type=MESH)
 
+    for way in range(2):
+        @pl.when(has[way])
+        def _():
+            for col in (1, 0):
+                coef_message(way, col).start()
     for half in range(HALVES):
         for way in range(2):
             @pl.when(has[way])
             def _():
-                for j in range(2):
-                    start_message(way, j, half).start()
-                    if half == 0:
-                        coef_message(way, j).start()
+                for col in (1, 0):
+                    start_message(way, col, half).start()
 
     def swap(src, dst, index):
         return pltpu.make_async_remote_copy(src, dst, side_send.at[index], side_recv.at[index], device_id={"col": other}, device_id_type=MESH)
 
     swaps = [
-        swap(c_hbm.at[1 - sys], c_raw.at[core], 0),
-        swap(f_hbm.at[1 - sys], res.at[:, pl.ds(mine, SUB), :], 1),
-        swap(u_hbm.at[1 - sys], cor.at[:, pl.ds(mine, SUB), :], 2),
-        swap(s_hbm.at[1 - sys], s_raw.at[core], 3),
+        swap(c_own.at[1 - sys], c_raw.at[core], 0),
+        swap(u_swap, cor.at[:, pl.ds(mine, SUB), :], 1),
+        swap(f_swap, res.at[:, pl.ds(mine, SUB), :], 2),
+        swap(si_swap, s_in.at[core], 3),
+        swap(so_swap, s_out.at[core], 4),
     ]
     for item in swaps:
         item.start()
@@ -222,7 +234,9 @@
         lane = pl.ds(half * width, width)
         to = (other, near[way])
         return (
-            pltpu.make_async_remote_copy(send_f.at[rnd, way, :, :, lane], recv_f.at[rnd, 1 - way, :, :, lane], fsend.at[rnd, way, half],
+            pltpu.make_async_remote_copy(send_f.at[rnd, way, 0, :, lane], recv_f.at[rnd, 1 - way, 0, :, lane], zsend.at[rnd, way, half],
+                                         zrecv.at[rnd, 1 - way, half], device_id=to, device_id_type=MESH),
+            pltpu.make_async_remote_copy(send_f.at[rnd, way, 1, :, lane], recv_f.at[rnd, 1 - way, 1, :, lane], fsend.at[rnd, way, half],
                                          frecv.at[rnd, 1 - way, half], device_id=to, device_id_type=MESH),
             pltpu.make_async_remote_copy(send_b.at[rnd, way, :, lane], recv_b.at[rnd, 1 - way, :, lane], bsend.at[rnd, way, half],
                                          brecv.at[rnd, 1 - way, half], device_id=to, device_id_type=MESH),
@@ -237,13 +251,12 @@
                 res[x, :, lanes] = first
                 res[y, :, lanes] = second
                 if rnd is not None:
-                    send_f[rnd, way, 0, :, lanes] = cor[x, :, lanes]
                     send_f[rnd, way, 1, :, lanes] = first
                     send_b[rnd, way, :, lanes] = second.astype(BF16)
             if rnd is not None:
                 @pl.when(has[way])
                 def _():
-                    for copy in message(rnd, way, half):
+                    for copy in message(rnd, way, half)[1:]:
                         copy.start()
 
     def update_inner(omega):
@@ -314,18 +327,18 @@
     for block in range(2):
         for x in range(SUB):
             app[block, x] = cor[x, SUB * block:SUB * (block + 1), :]
-    swaps[3].wait()
-    reorder(other)
+    for item in swaps[3:]:
+        item.wait()
     presolve()
 
     for way in range(2):
         @pl.when(has[way])
         def _():
             for block in range(2):
-                pltpu.make_async_remote_copy(c_own.at[block], c_nbr.at[way, block], csend.at[way, block], crecv.at[way, block],
+                pltpu.make_async_remote_copy(c_own.at[block, 0:8], c_nbr.at[way, block], csend.at[way, block], crecv.at[way, block],
                                              device_id=(other, near[way]), device_id_type=MESH).wait_recv()
         own = c_wide[EDGE_ROW[way]]
-        beyond = [jnp.concatenate([column(c_nbr, (way, block), x) for block in range(2)], axis=0) for x in (EDGE_ROW[1 - way], SECOND_ROW[1 - way])]
+        beyond = [jnp.concatenate([column(c_nbr, (way, block), x) for block in range(2)], axis=0) for x in ((7, 6) if way == 0 else (0, 1))]
         face_x[0 if way == 0 else SUB] = 0.5 * (own + jnp.where(has[way], beyond[0], own))
         for i in range(2):
             cross[way, i] = jnp.where(cell == SUB, 0.5 * (beyond[i] + pltpu.roll(beyond[i], 1, 0)), 0.0)
@@ -340,6 +353,12 @@
                 part = solve(block, 0, lanes)
                 for i, x in enumerate(EDGE_ROWS):
                     cor[x, SUB * block:SUB * (block + 1), lanes] = part[SUB * i:SUB * (i + 1)]
+                    if x in EDGE_ROW:
+                        send_f[sweep, EDGE_ROW.index(x), 0, SUB * block:SUB * (block + 1), lanes] = part[SUB * i:SUB * (i + 1)]
+            for way in range(2):
+                @pl.when(has[way])
+                def _():
+                    message(sweep, way, half)[0].start()
             update_edges(omega, half, sweep)
         for block in range(2):
             for x in EDGE_ROWS:
@@ -353,29 +372,43 @@
         update_inner(omega)
         presolve()
 
+    for at in range(0, CELLS, CHUNK):
+        for i, x in enumerate(rows_of(at)):
+            here = slice(at + SUB * i, at + SUB * (i + 1))
+            fin[x] = app[other, x] + omega * pre[other, here]
+    early = pltpu.make_async_remote_copy(fin, fin_recv, back_send.at[HALVES], back_recv.at[HALVES], device_id={"col": other}, device_id_type=MESH)
+    early.start()
+
     def back(half):
         lane = pl.ds(half * width, width)
-        return pltpu.make_async_remote_copy(fin.at[:, :, lane], out_ref.at[sys, :, :, lane], back_send.at[half], back_recv.at[half],
+        return pltpu.make_async_remote_copy(w_out.at[other, :, lane], w_fin.at[:, lane], back_send.at[half], back_recv.at[half],
                                             device_id={"col": other}, device_id_type=MESH)
 
-    for half in range(HALVES):
+    def finish_own(half):
         lanes = slice(half * width, (half + 1) * width)
-        take_edges(SWEEPS - 1, half, omega)
         for at in range(0, CELLS, CHUNK):
-            part = solve(other, at, lanes)
+            part = solve(core, at, lanes)
             for i, x in enumerate(rows_of(at)):
-                fin[x, :, lanes] = app[other, x, :, lanes] + omega * part[SUB * i:SUB * (i + 1)]
-        back(half).start()
-    for at in range(0, CELLS, CHUNK):
-        part = solve(core, at, slice(0, RHS))
-        for i, x in enumerate(rows_of(at)):
-            out_ref[sys, x] = app[core, x] + omega * part[SUB * i:SUB * (i + 1)]
-
-    for half in range(HALVES):
-        back(half).wait_send()
-        lane = pl.ds(half * width, width)
-        pltpu.make_async_remote_copy(fin.at[:, :, lane], out_ref.at[1 - sys, :, :, lane], back_send.at[half], back_recv.at[half],
-                                     device_id={"col": other}, device_id_type=MESH).wait_recv()
+                out_ref[sys, x, :, lanes] = app[core, x, :, lanes] + omega * part[SUB * i:SUB * (i + 1)]
+
+    def finish_other(half):
+        lanes = slice(half * width, (half + 1) * width)
+        back(half).wait()
+        for at in range(0, CELLS, CHUNK):
+            part = jnp.dot(so_swap[at:at + CHUNK], w_fin[:, lanes], preferred_element_type=F32)
+            for i, x in enumerate(rows_of(at)):
+                out_ref[1 - sys, x, :, lanes] = fin_recv[x, :, lanes] + their_omega * part[SUB * i:SUB * (i + 1)]
+
+    their_omega = om_ref[1 - sys]
+    take_edges(SWEEPS - 1, 0, omega)
+    back(0).start()
+    take_edges(SWEEPS - 1, 1, omega)
+    back(1).start()
+    finish_own(0)
+    finish_own(1)
+    early.wait()
+    finish_other(0)
+    finish_other(1)
     for way in range(2):
         @pl.when(has[way])
         def _():
@@ -418,7 +451,7 @@
                 pltpu.VMEM((2, INNER * SLOT, RHS), BF16),
                 pltpu.VMEM((2, SUB, SUB), F32),
                 pltpu.VMEM((2, SUB, SUB), F32),
-                pltpu.VMEM((2, 2, SUB, SUB), F32),
+                pltpu.VMEM((2, 2, 8, SUB), F32),
                 pltpu.VMEM(wide, F32),
                 pltpu.VMEM((2, SUB, SUB, LANES), F32),
                 pltpu.VMEM((SUB + 1, BAND, LANES), F32),
@@ -428,15 +461,21 @@
                 pltpu.VMEM(wide, F32),
                 pltpu.VMEM((2, 2, 3, SUB, RHS), F32),
                 pltpu.VMEM((2, 2, 2, SUB, RHS), F32),
+                pltpu.VMEM((SUB, SUB, RHS), F32),
+                pltpu.VMEM((SUB, SUB, RHS), F32),
+                pltpu.VMEM((CELLS, OUTER * SLOT), BF16),
+                pltpu.VMEM((CELLS, INNER * SLOT), BF16),
+                pltpu.VMEM((OUTER * SLOT, RHS), BF16),
+                pltpu.VMEM((SUB, SUB, RHS), F32),
                 pltpu.VMEM((2, 2, FIRST, RHS), F32),
                 pltpu.VMEM((2, 2, FIRST, RHS), F32),
                 pltpu.VMEM((rounds, 2, 2, BAND, RHS), F32),
                 pltpu.VMEM((rounds, 2, BAND, RHS), BF16),
                 pltpu.VMEM((rounds, 2, 2, BAND, RHS), F32),
                 pltpu.VMEM((rounds, 2, BAND, RHS), BF16),
-                dma((5,)), dma((2, 2, 2)), dma((4,)), dma((4,)), dma((2, 2)), dma((2, 2)), dma((2, 2, HALVES)), dma((2, 2, HALVES)),
-                dma((rounds, 2, HALVES)), dma((rounds, 2, HALVES)), dma((rounds, 2, HALVES)), dma((rounds, 2, HALVES)),
-                dma((HALVES,)), dma((HALVES,)),
+                dma((6,)), dma((2,)), dma((2, 2, 2)), dma((5,)), dma((5,)), dma((2, 2)), dma((2, 2)), dma((2, 2, HALVES)), dma((2, 2, HALVES)),
+                *[dma((rounds, 2, HALVES))] * 6,
+                dma((HALVES + 1,)), dma((HALVES + 1,)),
             ],
             compiler_params=pltpu.CompilerParams(collective_id=0, has_side_effects=True, vmem_limit_bytes=40 * 1024 * 1024),
         )(*held)

time: 34.9 us -> 34 us (0.974)
  Pallas kernels: 33.7 us -> 32.9 us
    pallas_call x1, Pallas kernels: 33.7 us -> 32.9 us  [local_sweeps(): pl.pallas_call(functools.partial(kernel, rows), out_shape=jax.ShapeDtypeS...]
where the time goes in v3:
time: 34 us; the launch traced here: 33.9 us
  Pallas kernels  32.9 us (97%)
  local copies, waits for them, and re-layouts  1.02 us (3%)
    pallas_call x1, Pallas kernels, local_sweeps(): pl.pallas_call(functools.partial(kernel, rows), out_shape=jax.ShapeDtypeS...  32.9 us
    unnamed x1, local copies, waits for them, and re-layouts  1.02 us

profile of v3, /device:TPU:97, one launch (start us, length us, event | category | flops | bytes accessed | tf_op | source)
XLA Modules:
  0.0 33.9 jit_solution(3021611126193640584)
XLA Ops:
  0.0 32.9 %shard_map.55 = f32[2,24,24,256]{3,2,1,0:T(8,128)S(1)} custom-call(f32[2,24,24,256]{3,2,1,0:T(8,128)} %f_hbm.1, f32[2,24,24,256]{3,2,1,0:T(8,128)} %u_hbm.1, f32[2,24,24]{2,1,0:T(8,128)} %c_hbm.1, bf16[2,784,576]{2,1,0:T(8,128)(2,1)} %bitcast.3, f32[2]{0:T(128)} %om_ref.1), custom_call_target="tpu_custom_call" | custom-call | tf_op jit(solution)/shard_map/pallas_call | solution.py:436
  32.9 1.0 %copy.7 = f32[2,24,24,256]{3,2,1,0:T(8,128)} copy(f32[2,24,24,256]{3,2,1,0:T(8,128)S(1)} %shard_map.55) | data formatting | bytes 2359296

commit v4 on v3

--- a/solution.py
+++ b/solution.py
@@ -30,12 +30,12 @@
 EDGE_ROW = (0, SUB - 1)
 SECOND_ROW = (1, SUB - 2)
 PLACES = ((0, 1, 2, 3), (7, 6, 5, 4))
-FIRST = 80
+FIRST = 2 * SUB + 8
 
 
 def kernel(rows, f_hbm, u_hbm, c_hbm, s_hbm, om_ref, out_ref, res, cor, app, fin, pre, s_raw, s_out, s_in, w_out, w_in, c_own, c_raw, c_nbr,
-           c_wide, c_part, face_x, face_lo, face_hi, cross, diag, u_edge, f_edge, f_swap, u_swap, so_swap, si_swap, w_fin, fin_recv, send_0, recv_0, send_f, send_b, recv_f, recv_b,
-           loc_sem, s_sem, edge_sem, side_send, side_recv, csend, crecv, send0_sem, recv0_sem, zsend, zrecv, fsend, frecv, bsend, brecv, back_send, back_recv):
+           c_wide, c_part, face_x, face_lo, face_hi, cross, diag, u_edge, f_edge, f_swap, u_swap, so_swap, si_swap, w_fin, fin_recv, send_0, recv_0, low_0, take_0, send_f, send_b, recv_f, recv_b,
+           loc_sem, s_sem, edge_sem, side_send, side_recv, csend, crecv, send0_sem, recv0_sem, low0_sem, take0_sem, zsend, zrecv, fsend, frecv, bsend, brecv, back_send, back_recv):
     core = lax.axis_index("col")
     row = lax.axis_index("row")
     other = 1 - core
@@ -43,6 +43,15 @@
     systems = (sys, 1 - sys)
     has = (row > 0, row < rows - 1)
     near = (jnp.maximum(row - 1, 0), jnp.minimum(row + 1, rows - 1))
+    slow = (lax.rem(row, 4) == 3).astype(jnp.int32)
+    slow_first = (slow, 1 - slow)
+
+    def present(way):
+        there = row + 2 * way - 1
+        return (there >= 0) & (there < rows)
+
+    def neighbour(way):
+        return jnp.clip(row + 2 * way - 1, 0, rows - 1)
     mine = pl.multiple_of(core * SUB, 8)
     width = RHS // HALVES
 
@@ -90,6 +99,7 @@
     for load in edge_loads:
         load.wait()
     spot = lax.broadcasted_iota(jnp.int32, (SUB, LANES), 0)
+    tile_row = lax.broadcasted_iota(jnp.int32, (8, LANES), 0)
     for j in range(2):
         for way in range(2):
             step = 1 if way == 0 else -1
@@ -110,11 +120,14 @@
                     flux = total * u[i] - lo * pltpu.roll(u[i], 1, 0) - hi * pltpu.roll(u[i], SUB - 1, 0) - link[i] * u[i + 1]
                     if i == 1:
                         flux = flux - link[0] * u[0]
-                    send_0[way, j, SUB * (i + 1):SUB * (i + 2), lanes] = f_edge[j, way, into[i], :, lanes] - flux
+                    part = f_edge[j, way, into[i], :, lanes] - flux
                     if i == 0:
                         send_0[way, j, 0:SUB, lanes] = u[0]
-            tile = jnp.where(core == 0, u_edge[j, way, place[1], SUB - 8:SUB, :], u_edge[j, way, place[1], 0:8, :])
-            send_0[way, j, 3 * SUB:FIRST, :] = tile
+                        send_0[way, j, SUB:2 * SUB, lanes] = part
+                    else:
+                        low_0[way, j, :, lanes] = part.astype(BF16)
+                        ends = [jnp.where(core == 0, v[SUB - 1:SUB], v[0:1]) for v in (u[1], part)]
+                        send_0[way, j, 2 * SUB:FIRST, lanes] = jnp.where(tile_row == 0, ends[0], ends[1])
 
     source = lax.broadcasted_iota(jnp.int32, (4 * EXT, 4 * SLOT), 0)
     target = lax.broadcasted_iota(jnp.int32, (4 * EXT, 4 * SLOT), 1)
@@ -151,8 +164,13 @@
     def start_message(way, col, half):
         lane = pl.ds(half * width, width)
         j = other if col == 0 else core
-        return pltpu.make_async_remote_copy(send_0.at[way, j, :, lane], recv_0.at[1 - way, core, :, lane], send0_sem.at[way, col, half],
-                                            recv0_sem.at[1 - way, core, half], device_id=(col, near[way]), device_id_type=MESH)
+        to = (col, near[way])
+        return (
+            pltpu.make_async_remote_copy(send_0.at[way, j, :, lane], recv_0.at[1 - way, core, :, lane], send0_sem.at[way, col, half],
+                                         recv0_sem.at[1 - way, core, half], device_id=to, device_id_type=MESH),
+            pltpu.make_async_remote_copy(low_0.at[way, j, :, lane], take_0.at[1 - way, core, :, lane], low0_sem.at[way, col, half],
+                                         take0_sem.at[1 - way, core, half], device_id=to, device_id_type=MESH),
+        )
 
     def coef_message(way, col):
         there = lax.rem(sys + (other if col == 0 else core), 2)
@@ -165,12 +183,13 @@
         def _():
             for col in (1, 0):
                 coef_message(way, col).start()
-    for half in range(HALVES):
-        for way in range(2):
-            @pl.when(has[way])
-            def _():
-                for col in (1, 0):
-                    start_message(way, col, half).start()
+    for col in (1, 0):
+        for half in range(HALVES):
+            for way in range(2):
+                @pl.when(has[way])
+                def _():
+                    for copy in start_message(way, col, half):
+                        copy.start()
 
     def swap(src, dst, index):
         return pltpu.make_async_remote_copy(src, dst, side_send.at[index], side_recv.at[index], device_id={"col": other}, device_id_type=MESH)
@@ -189,6 +208,7 @@
         @pl.when(jnp.logical_not(has[way]))
         def _():
             recv_0[way] = jnp.zeros(recv_0.shape[1:], F32)
+            take_0[way] = jnp.zeros(take_0.shape[1:], BF16)
             c_nbr[way] = jnp.zeros(c_nbr.shape[1:], F32)
             for rnd in range(SWEEPS - 1):
                 recv_f[rnd, way] = jnp.zeros(recv_f.shape[2:], F32)
@@ -215,13 +235,11 @@
             total = total + 0.5 * (own + c_wide[x + 1])
         diag[x] = total
 
-    def neighbourless(x, lanes, static=False):
+    def neighbourless(x, lanes, links):
         here = cor[x, :, lanes]
         flux = diag[x] * here - face_lo[x] * pltpu.roll(here, 1, 0) - face_hi[x] * pltpu.roll(here, BAND - 1, 0)
-        if not static or x > 0:
-            flux = flux - face_x[x] * cor[x - 1, :, lanes]
-        if not static or x < SUB - 1:
-            flux = flux - face_x[x + 1] * cor[x + 1, :, lanes]
+        for to, face in links:
+            flux = flux - face_x[face] * cor[to, :, lanes]
         return flux
 
     def put(window, place, lanes, values):
@@ -232,7 +250,7 @@
 
     def message(rnd, way, half):
         lane = pl.ds(half * width, width)
-        to = (other, near[way])
+        to = (other, neighbour(way))
         return (
             pltpu.make_async_remote_copy(send_f.at[rnd, way, 0, :, lane], recv_f.at[rnd, 1 - way, 0, :, lane], zsend.at[rnd, way, half],
                                          zrecv.at[rnd, 1 - way, half], device_id=to, device_id_type=MESH),
@@ -243,18 +261,19 @@
         )
 
     def update_edges(omega, half, rnd=None):
-        for way in range(2):
-            x, y = EDGE_ROW[way], SECOND_ROW[way]
+        for way in slow_first:
+            x, y, third = (SUB - 1) * way, 1 + (SUB - 3) * way, 2 + (SUB - 5) * way
+            link, next_link = 1 + (SUB - 2) * way, 2 + (SUB - 4) * way
             for lanes in lanes_of(half):
-                first = res[x, :, lanes] - omega * neighbourless(x, lanes, True)
-                second = res[y, :, lanes] - omega * neighbourless(y, lanes, True)
+                first = res[x, :, lanes] - omega * neighbourless(x, lanes, ((y, link),))
+                second = res[y, :, lanes] - omega * neighbourless(y, lanes, ((x, link), (third, next_link)))
                 res[x, :, lanes] = first
                 res[y, :, lanes] = second
                 if rnd is not None:
                     send_f[rnd, way, 1, :, lanes] = first
                     send_b[rnd, way, :, lanes] = second.astype(BF16)
             if rnd is not None:
-                @pl.when(has[way])
+                @pl.when(present(way))
                 def _():
                     for copy in message(rnd, way, half)[1:]:
                         copy.start()
@@ -262,7 +281,7 @@
     def update_inner(omega):
         def body(x, carry):
             for lanes in all_lanes:
-                new = res[x, :, lanes] - omega * neighbourless(x, lanes)
+                new = res[x, :, lanes] - omega * neighbourless(x, lanes, ((x - 1, x), (x + 1, x + 1)))
                 res[x, :, lanes] = new
                 put(w_in, x - 2, lanes, new)
             return carry
@@ -277,29 +296,30 @@
                 pre[block, part:part + CHUNK] = jnp.dot(s_in[block, part:part + CHUNK], w_in[block], preferred_element_type=F32)
 
     def take_edges(rnd, half, omega):
-        for way in range(2):
-            @pl.when(has[way])
+        for way in (1 - slow, slow):
+            @pl.when(present(way))
             def _():
                 if rnd == 0:
                     for block in range(2):
                         lane = pl.ds(half * width, width)
                         pltpu.make_async_remote_copy(send_0.at[way, block, :, lane], recv_0.at[way, block, :, lane], send0_sem.at[way, block, half],
-                                                     recv0_sem.at[way, block, half], device_id=(other, near[way]), device_id_type=MESH).wait_recv()
+                                                     recv0_sem.at[way, block, half], device_id=(other, neighbour(way)), device_id_type=MESH).wait_recv()
+                        pltpu.make_async_remote_copy(low_0.at[way, block, :, lane], take_0.at[way, block, :, lane], low0_sem.at[way, block, half],
+                                                     take0_sem.at[way, block, half], device_id=(other, neighbour(way)), device_id_type=MESH).wait_recv()
                 else:
                     for copy in message(rnd - 1, 1 - way, half):
                         copy.wait_recv()
-        for way in range(2):
-            x = EDGE_ROW[way]
-            face = face_x[0] if way == 0 else face_x[SUB]
+            x = (SUB - 1) * way
+            face = face_x[SUB * way]
             for lanes in lanes_of(half):
                 if rnd == 0:
-                    z_far, r_far, r_beyond = [jnp.concatenate([recv_0[way, block, SUB * i:SUB * (i + 1), lanes] for block in range(2)], axis=0) for i in range(3)]
-                    none = jnp.zeros((SUB - 8, LANES), F32)
-                    z_beyond = jnp.concatenate([none] + [recv_0[way, block, 3 * SUB:FIRST, lanes] for block in range(2)] + [none], axis=0)
+                    z_far, r_far = [jnp.concatenate([recv_0[way, block, SUB * i:SUB * (i + 1), lanes] for block in range(2)], axis=0) for i in range(2)]
                     side = cross[way, 0] * (z_far - pltpu.roll(z_far, 1, 0))
                     r_far = r_far - side + pltpu.roll(side, BAND - 1, 0)
-                    side = cross[way, 1] * (z_beyond - pltpu.roll(z_beyond, 1, 0))
-                    r_beyond = r_beyond - side + pltpu.roll(side, BAND - 1, 0)
+                    z_ends, r_ends = [[recv_0[way, block, 2 * SUB + i:2 * SUB + i + 1, lanes] for block in range(2)] for i in range(2)]
+                    side = cross[way, 1, SUB:SUB + 1, :] * (z_ends[1] - z_ends[0])
+                    r_beyond = jnp.concatenate([take_0[way, block, :, lanes].astype(F32) for block in range(2)], axis=0)
+                    r_beyond = jnp.where(cell == SUB - 1, r_ends[0] + side, jnp.where(cell == SUB, r_ends[1] - side, r_beyond))
                 else:
                     z_far = recv_f[rnd - 1, way, 0, :, lanes]
                     r_far = recv_f[rnd - 1, way, 1, :, lanes]
@@ -307,9 +327,9 @@
                 flux = omega * face * (cor[x, :, lanes] - z_far)
                 new = res[x, :, lanes] - flux
                 res[x, :, lanes] = new
-                put(w_out, PLACES[way][0], lanes, r_beyond)
-                put(w_out, PLACES[way][1], lanes, r_far + flux)
-                put(w_out, PLACES[way][2], lanes, new)
+                put(w_out, 7 * way, lanes, r_beyond)
+                put(w_out, 1 + 5 * way, lanes, r_far + flux)
+                put(w_out, 2 + 3 * way, lanes, new)
 
     def solve(block, part, lanes):
         return pre[block, part:part + CHUNK, lanes] + jnp.dot(s_out[block, part:part + CHUNK], w_out[block, :, lanes], preferred_element_type=F32)
@@ -355,8 +375,8 @@
                     cor[x, SUB * block:SUB * (block + 1), lanes] = part[SUB * i:SUB * (i + 1)]
                     if x in EDGE_ROW:
                         send_f[sweep, EDGE_ROW.index(x), 0, SUB * block:SUB * (block + 1), lanes] = part[SUB * i:SUB * (i + 1)]
-            for way in range(2):
-                @pl.when(has[way])
+            for way in slow_first:
+                @pl.when(present(way))
                 def _():
                     message(sweep, way, half)[0].start()
             update_edges(omega, half, sweep)
@@ -416,7 +436,8 @@
                 coef_message(way, j).wait_send()
             for half in range(HALVES):
                 for j in range(2):
-                    start_message(way, j, half).wait_send()
+                    for copy in start_message(way, j, half):
+                        copy.wait_send()
                 for rnd in range(SWEEPS - 1):
                     for copy in message(rnd, way, half):
                         copy.wait_send()
@@ -469,11 +490,13 @@
                 pltpu.VMEM((SUB, SUB, RHS), F32),
                 pltpu.VMEM((2, 2, FIRST, RHS), F32),
                 pltpu.VMEM((2, 2, FIRST, RHS), F32),
+                pltpu.VMEM((2, 2, SUB, RHS), BF16),
+                pltpu.VMEM((2, 2, SUB, RHS), BF16),
                 pltpu.VMEM((rounds, 2, 2, BAND, RHS), F32),
                 pltpu.VMEM((rounds, 2, BAND, RHS), BF16),
                 pltpu.VMEM((rounds, 2, 2, BAND, RHS), F32),
                 pltpu.VMEM((rounds, 2, BAND, RHS), BF16),
-                dma((6,)), dma((2,)), dma((2, 2, 2)), dma((5,)), dma((5,)), dma((2, 2)), dma((2, 2)), dma((2, 2, HALVES)), dma((2, 2, HALVES)),
+                dma((6,)), dma((2,)), dma((2, 2, 2)), dma((5,)), dma((5,)), dma((2, 2)), dma((2, 2)), *[dma((2, 2, HALVES))] * 4,
                 *[dma((rounds, 2, HALVES))] * 6,
                 dma((HALVES + 1,)), dma((HALVES + 1,)),
             ],

time: 34 us -> 33.4 us (0.982)
  Pallas kernels: 32.9 us -> 32.3 us
    pallas_call x1, Pallas kernels: 32.9 us -> 32.3 us  [local_sweeps(): pl.pallas_call(functools.partial(kernel, rows), out_shape=jax.ShapeDtypeS...]
where the time goes in v4:
time: 33.4 us; the launch traced here: 33.3 us
  Pallas kernels  32.3 us (97%)
  local copies, waits for them, and re-layouts  1.02 us (3%)
    pallas_call x1, Pallas kernels, local_sweeps(): pl.pallas_call(functools.partial(kernel, rows), out_shape=jax.ShapeDtypeS...  32.3 us
    unnamed x1, local copies, waits for them, and re-layouts  1.02 us

profile of v4, /device:TPU:97, one launch (start us, length us, event | category | flops | bytes accessed | tf_op | source)
XLA Modules:
  0.0 33.3 jit_solution(4170942633639533048)
XLA Ops:
  0.0 32.3 %shard_map.55 = f32[2,24,24,256]{3,2,1,0:T(8,128)S(1)} custom-call(f32[2,24,24,256]{3,2,1,0:T(8,128)} %f_hbm.1, f32[2,24,24,256]{3,2,1,0:T(8,128)} %u_hbm.1, f32[2,24,24]{2,1,0:T(8,128)} %c_hbm.1, bf16[2,784,576]{2,1,0:T(8,128)(2,1)} %bitcast.3, f32[2]{0:T(128)} %om_ref.1), custom_call_target="tpu_custom_call" | custom-call | tf_op jit(solution)/shard_map/pallas_call | solution.py:457
  32.3 1.0 %copy.7 = f32[2,24,24,256]{3,2,1,0:T(8,128)} copy(f32[2,24,24,256]{3,2,1,0:T(8,128)S(1)} %shard_map.55) | data formatting | bytes 2359296

commit v5 on v4

--- a/solution.py
+++ b/solution.py
@@ -83,7 +83,7 @@
         @pl.when(has[way])
         def _():
             for col in range(2):
-                pl.semaphore_signal(barrier, inc=1, device_id=(col, near[way]), device_id_type=MESH)
+                pl.semaphore_signal(barrier, inc=1, device_id=(col, neighbour(way)), device_id_type=MESH)
     pl.semaphore_signal(barrier, inc=1, device_id={"col": other}, device_id_type=MESH)
 
     eye = lax.broadcasted_iota(jnp.int32, (SUB, SUB), 0) == lax.broadcasted_iota(jnp.int32, (SUB, SUB), 1)
@@ -164,7 +164,7 @@
     def start_message(way, col, half):
         lane = pl.ds(half * width, width)
         j = other if col == 0 else core
-        to = (col, near[way])
+        to = (col, neighbour(way))
         return (
             pltpu.make_async_remote_copy(send_0.at[way, j, :, lane], recv_0.at[1 - way, core, :, lane], send0_sem.at[way, col, half],
                                          recv0_sem.at[1 - way, core, half], device_id=to, device_id_type=MESH),
@@ -176,18 +176,15 @@
         there = lax.rem(sys + (other if col == 0 else core), 2)
         tile = pl.ds((SUB - 8) * way, 8)
         return pltpu.make_async_remote_copy(c_own.at[there, tile], c_nbr.at[1 - way, core], csend.at[way, col], crecv.at[1 - way, core],
-                                            device_id=(col, near[way]), device_id_type=MESH)
-
-    for way in range(2):
-        @pl.when(has[way])
-        def _():
-            for col in (1, 0):
-                coef_message(way, col).start()
+                                            device_id=(col, neighbour(way)), device_id_type=MESH)
+
     for col in (1, 0):
         for half in range(HALVES):
-            for way in range(2):
-                @pl.when(has[way])
+            for way in slow_first:
+                @pl.when(present(way))
                 def _():
+                    if half == 0:
+                        coef_message(way, col).start()
                     for copy in start_message(way, col, half):
                         copy.start()
 

time: 33.4 us -> 33.2 us (level)
  no operation moved by 1% of the time
where the time goes in v5:
time: 33.2 us; the launch traced here: 33.1 us
  Pallas kernels  32.1 us (97%)
  local copies, waits for them, and re-layouts  1.02 us (3%)
    pallas_call x1, Pallas kernels, local_sweeps(): pl.pallas_call(functools.partial(kernel, rows), out_shape=jax.ShapeDtypeS...  32.1 us
    unnamed x1, local copies, waits for them, and re-layouts  1.02 us

profile of v5, /device:TPU:97, one launch (start us, length us, event | category | flops | bytes accessed | tf_op | source)
XLA Modules:
  0.0 33.1 jit_solution(17156764652380358876)
XLA Ops:
  0.0 32.1 %shard_map.55 = f32[2,24,24,256]{3,2,1,0:T(8,128)S(1)} custom-call(f32[2,24,24,256]{3,2,1,0:T(8,128)} %f_hbm.1, f32[2,24,24,256]{3,2,1,0:T(8,128)} %u_hbm.1, f32[2,24,24]{2,1,0:T(8,128)} %c_hbm.1, bf16[2,784,576]{2,1,0:T(8,128)(2,1)} %bitcast.3, f32[2]{0:T(128)} %om_ref.1), custom_call_target="tpu_custom_call" | custom-call | tf_op jit(solution)/shard_map/pallas_call | solution.py:454
  32.1 1.0 %copy.7 = f32[2,24,24,256]{3,2,1,0:T(8,128)} copy(f32[2,24,24,256]{3,2,1,0:T(8,128)S(1)} %shard_map.55) | data formatting | bytes 2359296
